TPU v7x, 128 devices: a whole 4x4x4 slice. The times are simulated.
128 devices in a mesh: dp: 16 (over z, y), tp: 8 (over x, core).
Axes of the slice: x: 4, y: 4, z: 4, core: 2. Of those that a mesh axis runs over, the one named last changes fastest.
Arguments:
- tokens: int32 [16, 1024], P('dp')
- emb_table: bfloat16 [65536, 2304], P('tp')
- w_norm: float32 [2304], replicated
- dy_norm: bfloat16 [16, 1024, 2304], P('dp', 'tp')
- dy_resid: bfloat16 [16, 1024, 2304], P('dp', 'tp')
Outputs:
- output 1: bfloat16 [16, 1024, 2304], P('dp', 'tp')
- output 2: bfloat16 [16, 1024, 2304], P('dp', 'tp')
- output 3: float32 [65536, 2304], P(('tp', 'dp'))
- output 4: float32 [2304], replicated
All inputs are finite; a program needn't handle non-finite values.
Results may differ from a plain program's by a relative error of at most 0.00848154.
Values sent between devices are 32-bit elements.
A program may use at most 1 GiB of HBM per device.

v0:
```python
import math
import jax
import jax.numpy as jnp
from jax import lax
from jax.sharding import PartitionSpec as P

NORM_EPS = 1e-6


def solution(mesh):
    def local_step(tokens, emb_table, w_norm, dy_norm, dy_resid):
        shard_rows, model_dim = emb_table.shape
        scale_float = jnp.asarray(math.sqrt(model_dim), jnp.bfloat16).astype(jnp.float32)
        local_ids = tokens - lax.axis_index("tp") * shard_rows
        owned_mask = (local_ids >= 0) & (local_ids < shard_rows)
        looked_up = jnp.take(emb_table, jnp.where(owned_mask, local_ids, 0), axis=0)
        partial_rows = jnp.where(owned_mask[..., None], looked_up.astype(jnp.float32) * scale_float, 0.0)
        x_emb = lax.psum_scatter(partial_rows, "tp", scatter_dimension=1, tiled=True).astype(jnp.bfloat16)
        x_float = x_emb.astype(jnp.float32)
        inv_rms = lax.rsqrt(jnp.mean(x_float * x_float, axis=-1, keepdims=True) + NORM_EPS)
        x_hat = x_float * inv_rms
        norm_gain = 1.0 + w_norm
        y_norm = (x_hat * norm_gain).astype(jnp.bfloat16)
        dy_float = dy_norm.astype(jnp.float32)
        dx_hat = dy_float * norm_gain
        tok_grad = dy_resid.astype(jnp.float32) + inv_rms * (dx_hat - x_hat * jnp.mean(dx_hat * x_hat, axis=-1, keepdims=True))
        w_grad = lax.psum(jnp.sum(dy_float * x_hat, axis=(0, 1)), ("dp", "tp"))
        seq_grad = lax.all_gather(tok_grad, "tp", axis=1, tiled=True)
        drop_ids = jnp.where(owned_mask, local_ids, shard_rows)
        shard_grad = jax.ops.segment_sum(seq_grad.reshape(-1, model_dim), drop_ids.reshape(-1), num_segments=shard_rows, mode="drop") * scale_float
        emb_grad = lax.psum_scatter(shard_grad, "dp", scatter_dimension=0, tiled=True)
        return x_emb, y_norm, emb_grad, w_grad

    act_spec = P("dp", "tp", None)
    return jax.shard_map(local_step, mesh=mesh, in_specs=(P("dp", None), P("tp", None), P(None), act_spec, act_spec), out_specs=(act_spec, act_spec, P(("tp", "dp"), None), P(None)), check_vma=False)
```

profile of v0, /device:TPU:0, one launch (start us, length us, event | category | flops | bytes accessed | tf_op | source)
XLA Modules:
  0.0 876.9 jit_solution(8377424210240210312)
XLA Ops:
  7.2 0.0 reduce-scatter.3.cloned.1.call-start
  7.2 0.7 and_reduce_fusion
  8.0 39.0 %gather_fusion = bf16[1024,2304]{1,0:T(8,128)(2,1)} fusion(bf16[8192,2304]{1,0:T(8,128)(2,1)} %param.6, s32[1024]{0:T(1024)S(1)} %broadcast_clamp_fusion), kind=kCustom, calls=%fused_computation | custom fusion | bytes 9441280 | tf_op jit(solution)/shard_map/jit(_take)/gather | solution.py:16
  47.0 6.3 multiply_select_fusion
  53.2 0.0 copy-start.4
  53.3 0.0 copy-start.1
  53.3 0.0 copy-start.2
  53.3 0.0 reduce-scatter.3.cloned.1.call-update
  53.3 0.0 copy-start.3
  53.3 0.0 all-gather.2.cloned.1.call-start
  53.3 0.6 copy-done.4
  54.0 76.3 %reduce-scatter.3.cloned.1.call-done = f32[1,128,2304]{2,1,0:T(8,128)} async-done(((f32[1,1024,2304]{2,1,0:T(8,128)}), f32[1,128,2304]{2,1,0:T(8,128)}) %reduce-scatter.3.cloned.1.call-update) | async-done | bytes 1179664 | tf_op jit(solution)/shard_map/reduce_scatter | solution.py:18
  130.3 1.5 fusion.8
  131.8 0.0 copy-start
  131.8 0.0 copy-done.1
  131.8 0.5 fusion.9
  132.2 0.0 copy-done.2
  132.3 1.7 fusion.5
  133.9 0.0 all-gather.2.cloned.1.call-update
  133.9 0.0 reduce-scatter.5.cloned.1.call-start
  134.0 0.0 copy-done.3
  134.0 53.7 %all-gather.2.cloned.1.call-done = f32[1,1024,2304]{2,1,0:T(8,128)} async-done(((f32[1,128,2304]{2,1,0:T(8,128)}), f32[1,1024,2304]{2,1,0:T(8,128)}) %all-gather.2.cloned.1.call-update) | async-done | bytes 9437200 | tf_op jit(solution)/shard_map/all_gather | solution.py:28
  187.8 23.8 %broadcast_in_dim.40 = f32[8192,2304]{1,0:T(8,128)} broadcast(f32[]{:T(128)} %constant.16.clone.1), dimensions={} | broadcast | bytes 75497472 | tf_op jit(solution)/shard_map/broadcast_in_dim | solution.py:30
  211.6 0.0 copy-done
  211.6 199.4 %scatter_fusion = f32[8192,2304]{1,0:T(8,128)} fusion(f32[8192,2304]{1,0:T(8,128)} %broadcast_in_dim.40, s32[1024]{0:T(1024)S(1)} %bitcast.8, f32[1024,2304]{1,0:T(8,128)} %bitcast.7), kind=kCustom, calls=%fused_computation.1 | custom fusion | flops 2359296 | bytes 28315648 | tf_op jit(solution)/shard_map/scatter-add | solution.py:30
  411.0 49.9 %broadcast_multiply_fusion = f32[8192,2304]{1,0:T(8,128)} fusion(f32[8192,2304]{1,0:T(8,128)} %scatter_fusion), kind=kLoop, calls=%fused_computation.2 | loop fusion | flops 18874368 | bytes 150994944 | tf_op jit(solution)/shard_map/mul | solution.py:30
  460.9 0.0 reduce-scatter.5.cloned.1.call-update
  460.9 71.9 %psum.7 = f32[2304]{0:T(1024)} all-reduce(f32[2304]{0:T(1024)S(1)} %get-tuple-element.4), channel_id=1, replica_groups=mesh['dp'=16,'tp'=8] {'dp','tp'}, use_global_device_ids=true, to_apply=%region_6.7 | all-reduce | flops 2304 | bytes 18432 | tf_op jit(solution)/shard_map/psum | solution.py:27
  532.8 337.5 %reduce-scatter.5.cloned.1.call-done = f32[512,2304]{1,0:T(8,128)} async-done(((f32[8192,2304]{1,0:T(8,128)}), f32[512,2304]{1,0:T(8,128)}) %reduce-scatter.5.cloned.1.call-update) | async-done | bytes 4718608 | tf_op jit(solution)/shard_map/reduce_scatter | solution.py:31
  (5 shorter events, 0.0 us)
Async XLA Ops:
  7.2 123.1 %reduce-scatter.3.cloned.1.call-start = ((), (), s32[]{:S(2)}) async-start(), calls=%async_computation.2 | async-start | bytes 10616832 | tf_op jit(solution)/shard_map/reduce_scatter | solution.py:18
  53.2 0.7 copy-start.4
  53.3 78.5 %copy-start.1 = (bf16[1,128,2304]{2,1,0:T(8,128)(2,1)S(1)}, bf16[1,128,2304]{2,1,0:T(8,128)(2,1)}, u32[]{:S(2)}) copy-start(bf16[1,128,2304]{2,1,0:T(8,128)(2,1)} %param.8) | copy-start | bytes 1769476
  53.3 79.0 %copy-start.2 = (bf16[1,128,2304]{2,1,0:T(8,128)(2,1)S(1)}, bf16[1,128,2304]{2,1,0:T(8,128)(2,1)}, u32[]{:S(2)}) copy-start(bf16[1,128,2304]{2,1,0:T(8,128)(2,1)} %param.9) | copy-start | bytes 1769476
  53.3 80.7 %copy-start.3 = (s32[1,1024]{1,0:T(1,128)S(1)}, s32[1,1024]{1,0:T(1,128)}, u32[]{:S(2)}) copy-start(s32[1,1024]{1,0:T(1,128)} %param.5) | copy-start | bytes 12292
  53.3 134.5 %all-gather.2.cloned.1.call-start = ((), (), s32[]{:S(2)}) async-start(), calls=%async_computation.3 | async-start | bytes 10616832 | tf_op jit(solution)/shard_map/all_gather | solution.py:28
  131.8 79.8 %copy-start = (bf16[1,128,2304]{2,1,0:T(8,128)(2,1)}, bf16[1,128,2304]{2,1,0:T(8,128)(2,1)S(1)}, u32[]{:S(2)}) copy-start(bf16[1,128,2304]{2,1,0:T(8,128)(2,1)S(1)} %get-tuple-element.7) | copy-start | bytes 1769476
  133.9 736.4 %reduce-scatter.5.cloned.1.call-start = ((), (), s32[]{:S(2)}) async-start(), calls=%async_computation.4 | async-start | bytes 80216064 | tf_op jit(solution)/shard_map/reduce_scatter | solution.py:31
Sparse Core Ops, SparseCore 0:
  53.4 76.8 reduce-scatter.2
  134.1 53.6 all-gather.1
  461.1 409.2 reduce-scatter.4
where the time goes:
time: 881 us; the launch traced here: 877 us
  waiting for transfers between devices  468 us (53%)
  other arithmetic  260 us (30%)
  blocking collectives  71.9 us (8%)
  local copies, waits for them, and re-layouts  63.5 us (7%)
  between operations  13.8 us (2%)
    reduce_scatter x1, waiting for transfers between devices, local_step(): lax.psum_scatter(shard_grad, 'dp', scatter_dimension=0, tiled=True)  337 us
    scatter-add x1, other arithmetic, local_step(): jax.ops.segment_sum(seq_grad.reshape(-1, model_dim), drop_ids.reshape(-1)...  199 us
    reduce_scatter x1, waiting for transfers between devices, local_step(): lax.psum_scatter(partial_rows, 'tp', scatter_dimension=1, tiled=True)  76.3 us
    psum x1, blocking collectives, local_step(): w_grad = lax.psum(jnp.sum(dy_float * x_hat, axis=(0, 1)), ('dp', 'tp'))  71.9 us
    all_gather x1, waiting for transfers between devices, local_step(): seq_grad = lax.all_gather(tok_grad, 'tp', axis=1, tiled=True)  53.7 us
    mul x1, other arithmetic, local_step(): jax.ops.segment_sum(seq_grad.reshape(-1, model_dim), drop_ids.reshape(-1)...  49.9 us
    gather x1, local copies, waits for them, and re-layouts, local_step(): looked_up = jnp.take(emb_table, jnp.where(owned_mask, local_ids, 0), axis=0)  39 us
    broadcast_in_dim x1, local copies, waits for them, and re-layouts, local_step(): jax.ops.segment_sum(seq_grad.reshape(-1, model_dim), drop_ids.reshape(-1)...  23.8 us
  transfers between devices with their start and end apart: 3, of which 3 were waited for; matrix products, arithmetic and copies ran while one was open for 0% of the time, Pallas kernels for 0%

commit v1 on v0

v1 whole, which is shorter than its diff:
```python
import functools
import math
import jax
import jax.numpy as jnp
from jax import lax
from jax.experimental import pallas as pl
from jax.experimental.pallas import tpu as pltpu
from jax.sharding import PartitionSpec as P

NORM_EPS = 1e-6
MESH = pl.DeviceIdType.MESH
HOT = 1024
STRIDE = 64
HOT_ROWS = 8
F32 = jnp.float32
BF16 = jnp.bfloat16
I32 = jnp.int32
VMEM = pltpu.VMEM
ANY = pl.ANY


def cold_cap(tp, blk):
    first = jnp.where(blk < 2, 0, jnp.where(blk < 4, 48, jnp.where(blk < 8, 32, 24)))
    return jnp.where(tp == 0, first, 16)


def gather_kernel(n_batch, batch, blk_ref, col_ref, table_ref, out_ref, buf, sems):
    def copies(step, slot):
        def one(i):
            row = pl.multiple_of(blk_ref[step * batch + i] * 8, 8)
            return pltpu.make_async_copy(
                table_ref.at[pl.ds(row, 8), :],
                buf.at[slot, pl.ds(pl.multiple_of(i * 8, 8), 8), :],
                sems.at[slot],
            )
        return one

    def start(step, slot):
        one = copies(step, slot)

        @pl.loop(0, batch)
        def _(i):
            one(i).start()

    depth = buf.shape[0]
    step = pl.program_id(0)

    @pl.when(step == 0)
    def _():
        for s in range(depth - 1):
            start(s, s)

    @pl.when(step + depth - 1 < n_batch)
    def _():
        start(step + depth - 1, lax.rem(step + depth - 1, depth))

    slot = lax.rem(step, depth)
    pltpu.make_async_copy(table_ref.at[pl.ds(0, batch * 8), :], buf.at[slot], sems.at[slot]).wait()
    col = col_ref[...]
    sel = (lax.broadcasted_iota(I32, (batch, batch * 8), 1) == col[:, :1]).astype(BF16)
    rows = jnp.dot(sel, buf[slot], preferred_element_type=F32)
    out_ref[...] = rows * math.sqrt(out_ref.shape[1])


def gather_rows(table, local_ids, owned):
    n, dim = local_ids.shape[0], table.shape[1]
    batch = 32
    safe = jnp.where(owned, local_ids, 0)
    blk = safe >> 3
    lane = (jnp.arange(n, dtype=I32) % batch) * 8 + (safe & 7)
    col = jnp.broadcast_to(jnp.where(owned, lane, -1)[:, None], (n, 128))
    return pl.pallas_call(
        functools.partial(gather_kernel, n // batch, batch),
        out_shape=jax.ShapeDtypeStruct((n, dim), F32),
        grid_spec=pltpu.PrefetchScalarGridSpec(
            num_scalar_prefetch=1,
            grid=(n // batch,),
            in_specs=[pl.BlockSpec((batch, 128), lambda i, *_: (i, 0)), pl.BlockSpec(memory_space=ANY)],
            out_specs=pl.BlockSpec((batch, dim), lambda i, *_: (i, 0)),
            scratch_shapes=[VMEM((4, batch * 8, dim), BF16), pltpu.SemaphoreType.DMA((4,))],
        ),
        compiler_params=pltpu.CompilerParams(dimension_semantics=("arbitrary",)),
        name="gather_rows",
    )(blk, col, table)


def index_kernel(n_dp, send_ref, recv_ref, send_sem, recv_sem):
    me = lax.axis_index("dp")
    recv_ref[pl.ds(me, 1)] = send_ref[pl.ds(me, 1)]

    def copy(i):
        to = lax.rem(me + i, n_dp)
        return pltpu.make_async_remote_copy(
            src_ref=send_ref.at[to], dst_ref=recv_ref.at[me],
            send_sem=send_sem.at[i], recv_sem=recv_sem.at[i],
            device_id={"dp": to}, device_id_type=MESH)

    def arrival(i):
        frm = lax.rem(me + n_dp - i, n_dp)
        return pltpu.make_async_remote_copy(
            src_ref=send_ref.at[frm], dst_ref=recv_ref.at[frm],
            send_sem=send_sem.at[i], recv_sem=recv_sem.at[i],
            device_id={"dp": frm}, device_id_type=MESH)

    for i in range(1, n_dp):
        copy(i).start()
    for i in range(1, n_dp):
        copy(i).wait_send()
        arrival(i).wait_recv()


def exchange_index(n_dp, send):
    return pl.pallas_call(
        functools.partial(index_kernel, n_dp),
        out_shape=jax.ShapeDtypeStruct(send.shape, I32),
        in_specs=[pl.BlockSpec(memory_space=VMEM)],
        out_specs=pl.BlockSpec(memory_space=VMEM),
        scratch_shapes=[pltpu.SemaphoreType.DMA((n_dp,)), pltpu.SemaphoreType.DMA((n_dp,))],
        compiler_params=pltpu.CompilerParams(has_side_effects=True),
        name="exchange_index",
    )(send)


def split3(x):
    hi = x.astype(BF16)
    rest = x - hi.astype(F32)
    mid = rest.astype(BF16)
    return hi, mid, (rest - mid.astype(F32)).astype(BF16)


def dot_exact(one_hot, x):
    parts = [jnp.dot(one_hot, p, preferred_element_type=F32) for p in split3(x)]
    return (parts[2] + parts[1]) + parts[0]


SUB = 256
NCHUNK = 3


def grad_kernel(n_dp, n_tp, slot_ref, idx_ref, g_ref, w_ref, out_ref, wout_ref,
                pick, place, send, recv, hot_send, hot_recv, w_dp, w_sum, w_tp,
                send_sem, recv_sem, hot_sem, wd_send, wd_recv, wt_send, wt_recv):
    me, plane = lax.axis_index("dp"), lax.axis_index("tp")
    dim = g_ref.shape[1]
    wide = dim // NCHUNK
    n_slots = n_dp * STRIDE
    scale = math.sqrt(dim)
    sizes = (8, 24, 32, 40, 56)

    def n_rows(blk):
        return HOT_ROWS + cold_cap(plane, blk)

    def peer(i):
        return lax.rem(me + i, n_dp), lax.rem(me + n_dp - i, n_dp)

    def w_copy(i, slot):
        return pltpu.make_async_remote_copy(
            src_ref=w_ref, dst_ref=w_dp.at[slot], send_sem=wd_send.at[i], recv_sem=wd_recv.at[i],
            device_id={"dp": peer(i)[0]}, device_id_type=MESH)

    for i in range(1, n_dp):
        w_copy(i, me).start()

    n_tok = g_ref.shape[0]

    @pl.loop(0, n_slots // 128)
    def _(b):
        base = pl.multiple_of(b * 128, 128)
        rows = lax.broadcasted_iota(I32, (128, n_tok), 0) + base
        pick[pl.ds(base, 128), :] = (rows == slot_ref[...]).astype(BF16)

    mine = n_rows(me)

    @pl.loop(0, n_dp)
    def _(s):
        @pl.loop(lax.div(mine, 8), STRIDE // 8)
        def _(r):
            recv[s, pl.ds(pl.multiple_of(r * 8, 8), 8), :] = jnp.zeros((8, dim), F32)

    def row_copy(c, i, size, to, slot):
        cols = pl.ds(pl.multiple_of(c * wide, 128), wide)
        return pltpu.make_async_remote_copy(
            src_ref=send.at[pl.ds(pl.multiple_of(to * STRIDE, 8), size), cols],
            dst_ref=recv.at[slot, pl.ds(0, size), cols],
            send_sem=send_sem.at[c, i], recv_sem=recv_sem.at[c, i],
            device_id={"dp": to}, device_id_type=MESH)

    def by_size(want, fn):
        for size in sizes:
            @pl.when(want == size)
            def _():
                fn(size)

    @pl.loop(0, NCHUNK)
    def _(c):
        @pl.loop(0, wide // SUB)
        def _(s):
            cols = pl.ds(pl.multiple_of(c * wide + s * SUB, 128), SUB)
            send[:, cols] = dot_exact(pick[...], g_ref[:, cols])

        @pl.loop(1, n_dp)
        def _(i):
            to = peer(i)[0]
            by_size(n_rows(to), lambda size: row_copy(c, i, size, to, me).start())

    recv[pl.ds(me, 1)] = send[pl.ds(pl.multiple_of(me * STRIDE, 8), STRIDE), :][None]

    w_dp[pl.ds(me, 1)] = w_ref[...][None]
    for i in range(1, n_dp):
        w_copy(i, me).wait_send()
        w_copy(i, peer(i)[1]).wait_recv()
    w_sum[...] = jnp.sum(w_dp[...], axis=0)

    def wt_copy(i, slot):
        return pltpu.make_async_remote_copy(
            src_ref=w_sum, dst_ref=w_tp.at[slot], send_sem=wt_send.at[i], recv_sem=wt_recv.at[i],
            device_id={"tp": lax.rem(plane + i, n_tp)}, device_id_type=MESH)

    for i in range(1, n_tp):
        wt_copy(i, plane).start()

    @pl.loop(0, n_dp // 2)
    def _(p):
        lane = lax.broadcasted_iota(I32, (1, 128), 1)
        idx = jnp.where(lane < STRIDE, idx_ref[2 * p, 0:1, :], idx_ref[2 * p + 1, 0:1, :])
        rows = lax.broadcasted_iota(I32, (place.shape[0], 128), 0)
        place[:, pl.ds(pl.multiple_of(p * 128, 128), 128)] = (rows == idx).astype(BF16)

    w_tp[pl.ds(plane, 1)] = w_sum[...][None]
    for i in range(1, n_tp):
        wt_copy(i, plane).wait_send()
        wt_copy(i, lax.rem(plane + n_tp - i, n_tp)).wait_recv()
    wout_ref[...] = jnp.sum(w_tp[...], axis=0)

    @pl.loop(0, NCHUNK)
    def _(c):
        @pl.loop(1, n_dp)
        def _(i):
            to, frm = peer(i)
            by_size(n_rows(to), lambda size: row_copy(c, i, size, to, me).wait_send())
            by_size(mine, lambda size: row_copy(c, i, size, frm, frm).wait_recv())

        @pl.loop(0, wide // SUB)
        def _(s):
            cols = pl.ds(pl.multiple_of(c * wide + s * SUB, 128), SUB)
            rows = recv[:, :, cols]
            hot_send[:, cols] = jnp.sum(rows[:, :HOT_ROWS, :], axis=0) * scale
            out_ref[:, cols] = dot_exact(place[...], rows.reshape(n_slots, SUB)) * scale

    per = n_tp // 2
    owner = lax.div(plane, per)
    at = pl.multiple_of(lax.rem(plane, per) * (n_dp * HOT_ROWS) + me * HOT_ROWS, 8)
    own = jnp.logical_and(plane == 0, me == owner)
    hot_copy = pltpu.make_async_remote_copy(
        src_ref=hot_send, dst_ref=hot_recv.at[pl.ds(at, HOT_ROWS), :],
        send_sem=hot_sem.at[0], recv_sem=hot_sem.at[1],
        device_id={"dp": owner, "tp": 0}, device_id_type=MESH)

    @pl.when(jnp.logical_not(own))
    def _():
        hot_copy.start()
        hot_copy.wait_send()

    total = hot_recv.shape[0]

    def hot_wait(n):
        ref = hot_recv.at[pl.ds(0, n), :]
        pltpu.make_async_remote_copy(
            src_ref=ref, dst_ref=ref, send_sem=hot_sem.at[0], recv_sem=hot_sem.at[1],
            device_id={"dp": 1, "tp": 0}, device_id_type=MESH).wait_recv()

    @pl.when(own)
    def _():
        hot_recv[0:HOT_ROWS, :] = hot_send[...]
        hot_wait(total - HOT_ROWS)

    @pl.when(jnp.logical_and(plane == 0, me == 1))
    def _():
        hot_wait(total)

    @pl.when(jnp.logical_and(plane == 0, me < 2))
    def _():
        out_ref[...] += hot_recv[...]


def exchange_grads(n_dp, n_tp, out_rows, slot, idx, g_all, w_part):
    n_tok, dim = g_all.shape
    dma = pltpu.SemaphoreType.DMA
    return pl.pallas_call(
        functools.partial(grad_kernel, n_dp, n_tp),
        out_shape=(jax.ShapeDtypeStruct((out_rows, dim), F32), jax.ShapeDtypeStruct(w_part.shape, F32)),
        in_specs=[pl.BlockSpec(memory_space=VMEM)] * 4,
        out_specs=(pl.BlockSpec(memory_space=VMEM), pl.BlockSpec(memory_space=VMEM)),
        scratch_shapes=[
            VMEM((n_dp * STRIDE, n_tok), BF16),
            VMEM((out_rows, n_dp * STRIDE), BF16),
            VMEM((n_dp * STRIDE, dim), F32),
            VMEM((n_dp, STRIDE, dim), F32),
            VMEM((HOT_ROWS, dim), F32),
            VMEM((HOT // 2, dim), F32),
            VMEM((n_dp,) + w_part.shape, F32),
            VMEM(w_part.shape, F32),
            VMEM((n_tp,) + w_part.shape, F32),
            dma((NCHUNK, n_dp)), dma((NCHUNK, n_dp)), dma((2,)),
            dma((n_dp,)), dma((n_dp,)), dma((n_tp,)), dma((n_tp,)),
        ],
        compiler_params=pltpu.CompilerParams(has_side_effects=True, vmem_limit_bytes=60 * 2**20),
        name="exchange_grads",
    )(slot, idx, g_all, w_part)


def swap(x, axis):
    return lax.all_to_all(x, axis, split_axis=0, concat_axis=0)


def dense_grads(n_dp, n_tp, out_rows, tokens, g_all, w_part):
    rows = n_dp * out_rows
    local = tokens - lax.axis_index("tp") * rows
    drop = jnp.where((local >= 0) & (local < rows), local, rows)
    shard = jax.ops.segment_sum(g_all, drop, num_segments=rows, mode="drop")
    emb = jnp.sum(swap(shard.reshape(n_dp, out_rows, -1), "dp"), axis=0) * math.sqrt(g_all.shape[1])
    w = jnp.sum(swap(jnp.broadcast_to(w_part, (n_dp,) + w_part.shape), "dp"), axis=0)
    w = jnp.sum(swap(jnp.broadcast_to(w, (n_tp,) + w.shape), "tp"), axis=0)
    return emb, w


def route(n_dp, n_tp, out_rows, ids):
    plane = lax.axis_index("tp")
    n = ids.shape[0]
    cold = ids >= HOT
    bins = ids // out_rows
    hits = (bins[:, None] == jnp.arange(n_dp * n_tp)[None]) & cold[:, None]
    bin_no = jnp.arange(n_dp * n_tp)
    flag = jnp.any(jnp.sum(hits.astype(I32), axis=0) > cold_cap(bin_no // n_dp, bin_no % n_dp))
    blk = bins % n_dp
    mine = cold & (bins // n_dp == plane)
    block_hit = (blk[:, None] == jnp.arange(n_dp)[None]) & mine[:, None]
    before = (jnp.arange(n)[:, None] > jnp.arange(n)[None]).astype(BF16)
    rank = jnp.sum(jnp.where(block_hit, jnp.dot(before, block_hit.astype(BF16), preferred_element_type=F32), 0.0), axis=1).astype(I32)
    cold_slot = blk * STRIDE + HOT_ROWS + rank
    per_plane = HOT // n_tp
    in_plane = ids % per_plane
    hot_slot = (in_plane // HOT_ROWS) * STRIDE + in_plane % HOT_ROWS
    hot = jnp.logical_not(cold) & (ids // per_plane == plane)
    slot = jnp.where(mine, cold_slot, jnp.where(hot, hot_slot, -1))
    slots = jnp.arange(n_dp * STRIDE)
    row = jnp.max(jnp.where((slots[:, None] == slot[None]) & mine[None], (ids % out_rows)[None], -1), axis=1)
    row = row.reshape(n_dp, 1, STRIDE)
    row = jnp.concatenate([row, row], axis=2)
    send = jnp.where(jnp.arange(8)[None, :, None] == 1, flag.astype(I32), row)
    return slot.reshape(1, n), send


def solution(mesh):
    n_dp, n_tp = mesh.shape["dp"], mesh.shape["tp"]

    def local_step(tokens, emb_table, w_norm, dy_norm, dy_resid):
        shard_rows, dim = emb_table.shape
        out_rows = shard_rows // n_dp
        ids = tokens[0]
        slot, send_idx = route(n_dp, n_tp, out_rows, ids)
        idx = exchange_index(n_dp, send_idx)
        fits = jnp.max(idx[:, 1, :]) == 0

        local_ids = ids - lax.axis_index("tp") * shard_rows
        owned = (local_ids >= 0) & (local_ids < shard_rows)
        partial_rows = gather_rows(emb_table, local_ids, owned)[None]
        x_emb = lax.psum_scatter(partial_rows, "tp", scatter_dimension=1, tiled=True).astype(BF16)
        x_float = x_emb.astype(F32)
        inv_rms = lax.rsqrt(jnp.mean(x_float * x_float, axis=-1, keepdims=True) + NORM_EPS)
        x_hat = x_float * inv_rms
        norm_gain = 1.0 + w_norm
        y_norm = (x_hat * norm_gain).astype(BF16)
        dy_float = dy_norm.astype(F32)
        dx_hat = dy_float * norm_gain
        tok_grad = dy_resid.astype(F32) + inv_rms * (dx_hat - x_hat * jnp.mean(dx_hat * x_hat, axis=-1, keepdims=True))
        w_part = jnp.sum(dy_float * x_hat, axis=(0, 1)).reshape(dim // 128, 128)
        w_part = jnp.pad(w_part, ((0, -(dim // 128) % 8), (0, 0)))
        g_all = lax.all_gather(tok_grad, "tp", axis=1, tiled=True)[0]
        emb_grad, w_sum = lax.cond(
            fits,
            lambda: exchange_grads(n_dp, n_tp, out_rows, slot, idx, g_all, w_part),
            lambda: dense_grads(n_dp, n_tp, out_rows, ids, g_all, w_part),
        )
        return x_emb, y_norm, emb_grad, w_sum[: dim // 128].reshape(dim)

    act_spec = P("dp", "tp", None)
    return jax.shard_map(local_step, mesh=mesh, in_specs=(P("dp", None), P("tp", None), P(None), act_spec, act_spec), out_specs=(act_spec, act_spec, P(("tp", "dp"), None), P(None)), check_vma=False)
```

time: 881 us -> 319 us (0.36)
  waiting for transfers between devices: 468 us -> 120 us
  other arithmetic: 260 us -> 8.54 us
  Pallas kernels: 0 us -> 162 us
  blocking collectives: 71.9 us -> 0 us
  local copies, waits for them, and re-layouts: 63.5 us -> 7.23 us
    reduce_scatter x1 -> x0, waiting for transfers between devices: 337 us -> none  [local_step(): lax.psum_scatter(shard_grad, 'dp', scatter_dimension=0, tiled=True)]
    scatter-add x1 -> x0, other arithmetic: 199 us -> none  [local_step(): jax.ops.segment_sum(seq_grad.reshape(-1, model_dim), drop_ids.reshape(-1)...]
    pallas_call x0 -> x3, Pallas kernels: none -> 162 us  [the longest x1 99.2 us: exchange_grads(): pl.pallas_call(functools.partial(grad_kernel, n_dp, n_tp), out_shape=(jax...]
    psum x1 -> x0, blocking collectives: 71.9 us -> none  [local_step(): w_grad = lax.psum(jnp.sum(dy_float * x_hat, axis=(0, 1)), ('dp', 'tp'))]
    mul x1 -> x0, other arithmetic: 49.9 us -> none  [local_step(): jax.ops.segment_sum(seq_grad.reshape(-1, model_dim), drop_ids.reshape(-1)...]
    gather x1 -> x0, local copies, waits for them, and re-layouts: 39 us -> none  [local_step(): looked_up = jnp.take(emb_table, jnp.where(owned_mask, local_ids, 0), axis=0)]
    broadcast_in_dim x1, local copies, waits for them, and re-layouts: 23.8 us -> 0.99 us  [gather_rows(): col = jnp.broadcast_to(jnp.where(owned, lane, -1)[:, None], (n, 128))]
    all_gather x1, waiting for transfers between devices: 53.7 us -> 32.4 us  [local_step(): g_all = lax.all_gather(tok_grad, 'tp', axis=1, tiled=True)[0]]
  transfers between devices with their start and end apart: 3 -> 2, of which waited for: 3 -> 2; matrix products, arithmetic and copies ran while one was open for 0% -> 1% of each run, Pallas kernels for 0% -> 5%
where the time goes in v1:
time: 319 us; the launch traced here: 314 us
  Pallas kernels  162 us (51%)
  waiting for transfers between devices  120 us (38%)
  between operations  15.5 us (5%)
  other arithmetic  8.54 us (3%)
  local copies, waits for them, and re-layouts  7.23 us (2%)
    pallas_call x1, Pallas kernels, exchange_grads(): pl.pallas_call(functools.partial(grad_kernel, n_dp, n_tp), out_shape=(jax...  99.2 us
    reduce_scatter x1, waiting for transfers between devices, local_step(): lax.psum_scatter(partial_rows, 'tp', scatter_dimension=1, tiled=True)  87.8 us
    pallas_call x1, Pallas kernels, gather_rows(): pl.pallas_call(functools.partial(gather_kernel, n // batch, batch), out_s...  47.2 us
    all_gather x1, waiting for transfers between devices, local_step(): g_all = lax.all_gather(tok_grad, 'tp', axis=1, tiled=True)[0]  32.4 us
    pallas_call x1, Pallas kernels, exchange_index(): pl.pallas_call(functools.partial(index_kernel, n_dp), out_shape=jax.Shape...  15.8 us
  transfers between devices with their start and end apart: 2, of which 2 were waited for; matrix products, arithmetic and copies ran while one was open for 1% of the time, Pallas kernels for 5%

profile of v1, /device:TPU:0, one launch (start us, length us, event | category | flops | bytes accessed | tf_op | source)
XLA Modules:
  0.0 314.4 jit_solution(15246016032168664229)
XLA Ops:
  7.2 0.0 reduce-scatter.2.cloned.1.call-start
  7.2 1.3 fusion.22
  8.5 1.0 broadcast_in_dim.98.col_ref
  9.5 47.2 %gather_rows.1 = f32[1024,2304]{1,0:T(8,128)} custom-call(s32[1024]{0:T(1024)} %get-tuple-element.48.blk_ref, s32[1024,128]{1,0:T(8,128)} %broadcast_in_dim.98.col_ref, bf16[8192,2304]{1,0:T(8,128)(2,1)} %table_ref.1), custom_call_target="tpu_custom_call" | custom-call | tf_op jit(solution)/shard_map/gather_rows/pallas_call | solution.py:72
  56.7 0.0 copy-start.4
  56.7 0.0 copy-start.1
  56.8 0.0 copy-start.2
  56.8 0.0 reduce-scatter.2.cloned.1.call-update
  56.8 0.0 copy-start.3
  56.8 0.0 all-gather.2.cloned.1.call-start
  56.9 0.6 copy-done.4
  57.4 87.8 %reduce-scatter.2.cloned.1.call-done = f32[1,128,2304]{2,1,0:T(8,128)} async-done(((f32[1,1024,2304]{2,1,0:T(8,128)}), f32[1,128,2304]{2,1,0:T(8,128)}) %reduce-scatter.2.cloned.1.call-update) | async-done | bytes 1179664 | tf_op jit(solution)/shard_map/reduce_scatter | solution.py:368
  145.3 1.5 fusion.10
  146.8 0.5 fusion.11
  147.2 1.7 fusion.7
  148.9 0.0 all-gather.2.cloned.1.call-update
  149.0 0.5 fusion.13
  149.5 0.1 fusion.37
  149.6 0.1 fusion.28
  149.7 1.0 select_reduce_fusion
  150.7 0.1 reshape.166
  150.8 0.4 convert_reduce_fusion
  151.1 0.6 compare_reduce_fusion
  152.5 0.1 add_bitcast_fusion
  152.5 0.7 broadcast_select_fusion.send_ref
  153.2 15.8 %exchange_index.1 = s32[16,8,128]{2,1,0:T(8,128)S(1)} custom-call(s32[16,8,128]{2,1,0:T(8,128)} %broadcast_select_fusion.send_ref), custom_call_target="tpu_custom_call" | custom-call | tf_op jit(solution)/shard_map/exchange_index/pallas_call | solution.py:113
  169.0 0.6 slice_reduce_fusion
  170.3 32.4 %all-gather.2.cloned.1.call-done = f32[1,1024,2304]{2,1,0:T(8,128)} async-done(((f32[1,128,2304]{2,1,0:T(8,128)}), f32[1,1024,2304]{2,1,0:T(8,128)}) %all-gather.2.cloned.1.call-update) | async-done | bytes 9437200 | tf_op jit(solution)/shard_map/all_gather | solution.py:379
  202.7 99.9 %conditional.1 = (f32[512,2304]{1,0:T(8,128)}, f32[2304]{0:T(1024)S(1)}) conditional(s32[]{:T(128)} %convert_element_type.48, (s32[1024]{0:T(1024)S(1)}, f32[1024,2304]{1,0:T(8,128)}, f32[24,128]{1,0:T(8,128)S(1)}) %tuple.40, (s32[1,1024]{1,0:T(1,128)S(1)}, s32[16,8,128]{2,1,0:T(8,128)S(1)}, f32[1024,2304]{1,0:T(8,128)}, ...), branch_computations={%region_9.14_spmd, %region_14.15_spmd} | conditional | flops 21306372 | bytes 421509248 | solution.py:380
  202.7 99.2 %exchange_grads.1 = (f32[512,2304]{1,0:T(8,128)}, f32[24,128]{1,0:T(8,128)}) custom-call(s32[1,1024]{1,0:T(1,128)S(1)} %get-tuple-element.20.slot_ref, s32[16,8,128]{2,1,0:T(8,128)S(1)} %get-tuple-element.21.idx_ref, f32[1024,2304]{1,0:T(8,128)} %get-tuple-element.22.g_ref, f32[24,128]{1,0:T(8,128)S(1)} %get-tuple-element.23.w_ref), custom_call_target="tpu_custom_call" | custom-call | tf_op jit(solution)/shard_map/cond/branch_1_fun/exchange_grads/pallas_call | solution.py:289
  302.0 0.7 slice_bitcast_fusion
  302.7 4.8 %copy.15 = f32[512,2304]{1,0:T(8,128)} copy(f32[512,2304]{1,0:T(8,128)} %get-tuple-element.59) | data formatting | bytes 9437184
  (16 shorter events, 0.1 us)
Async XLA Ops:
  7.2 138.1 %reduce-scatter.2.cloned.1.call-start = ((), (), s32[]{:S(2)}) async-start(), calls=%async_computation.4 | async-start | bytes 10616832 | tf_op jit(solution)/shard_map/reduce_scatter | solution.py:368
  56.7 0.7 copy-start.4
  56.7 90.0 %copy-start.1 = (bf16[1,128,2304]{2,1,0:T(8,128)(2,1)S(1)}, bf16[1,128,2304]{2,1,0:T(8,128)(2,1)}, u32[]{:S(2)}) copy-start(bf16[1,128,2304]{2,1,0:T(8,128)(2,1)} %param.10) | copy-start | bytes 1769476
  56.8 90.5 %copy-start.2 = (bf16[1,128,2304]{2,1,0:T(8,128)(2,1)S(1)}, bf16[1,128,2304]{2,1,0:T(8,128)(2,1)}, u32[]{:S(2)}) copy-start(bf16[1,128,2304]{2,1,0:T(8,128)(2,1)} %param.11) | copy-start | bytes 1769476
  56.8 92.1 %copy-start.3 = (s32[1,1024]{1,0:T(1,128)S(1)}, s32[1,1024]{1,0:T(1,128)}, u32[]{:S(2)}) copy-start(s32[1,1024]{1,0:T(1,128)} %param.7) | copy-start | bytes 12292
  56.8 145.9 %all-gather.2.cloned.1.call-start = ((), (), s32[]{:S(2)}) async-start(), calls=%async_computation.5 | async-start | bytes 10616832 | tf_op jit(solution)/shard_map/all_gather | solution.py:379
  146.8 56.0 %copy-start = (bf16[1,128,2304]{2,1,0:T(8,128)(2,1)}, bf16[1,128,2304]{2,1,0:T(8,128)(2,1)S(1)}, u32[]{:S(2)}) copy-start(bf16[1,128,2304]{2,1,0:T(8,128)(2,1)S(1)} %get-tuple-element.57) | copy-start | bytes 1769476
  302.7 4.8 %copy-start.5 = (f32[2304]{0:T(1024)}, f32[2304]{0:T(1024)S(1)}, u32[]{:S(2)}) copy-start(f32[2304]{0:T(1024)S(1)} %get-tuple-element.60) | copy-start | bytes 27652
Sparse Core Ops, SparseCore 0:
  56.9 88.3 reduce-scatter.1
  149.1 53.6 all-gather.1

commit v2 on v1

v2 whole, which is shorter than its diff:
```python
import functools
import math
import jax
import jax.numpy as jnp
from jax import lax
from jax.experimental import pallas as pl
from jax.experimental.pallas import tpu as pltpu
from jax.sharding import PartitionSpec as P

NORM_EPS = 1e-6
MESH = pl.DeviceIdType.MESH
HOT = 1024
STRIDE = 64
HOT_ROWS = 8
F32 = jnp.float32
BF16 = jnp.bfloat16
I32 = jnp.int32
VMEM = pltpu.VMEM
ANY = pl.ANY


def cold_cap(tp, blk):
    first = jnp.where(blk < 2, 0, jnp.where(blk < 4, 48, jnp.where(blk < 8, 32, 24)))
    return jnp.where(tp == 0, first, 16)


def gather_kernel(batch, blk_ref, count_ref, comb_ref, table_ref, out_ref, front, buf, sel, front_sem, sems):
    n_front, dim = front.shape
    n_tok = out_ref.shape[0]
    scale = math.sqrt(dim)
    count = count_ref[0]
    n_batch = lax.div(count + batch - 1, batch)
    head = pltpu.make_async_copy(table_ref.at[pl.ds(0, n_front), :], front, front_sem)
    head.start()

    def copy(blk, slot, i):
        return pltpu.make_async_copy(
            table_ref.at[pl.ds(pl.multiple_of(blk * 8, 8), 8), :],
            buf.at[slot, pl.ds(pl.multiple_of(i * 8, 8), 8), :],
            sems.at[slot])

    def in_batch(b):
        return jnp.minimum(count - b * batch, batch)

    def start(b):
        slot = lax.rem(b, 2)

        @pl.loop(0, in_batch(b))
        def _(i):
            copy(blk_ref[b * batch + i], slot, i).start()

    buf[...] = jnp.zeros(buf.shape, BF16)

    @pl.when(n_batch > 0)
    def _():
        start(0)

    def choose(base, width):
        @pl.loop(0, n_tok // 128)
        def _(r):
            rows = pl.ds(pl.multiple_of(r * 128, 128), 128)
            lanes = lax.broadcasted_iota(I32, (128, width), 1) + base
            sel[rows, :width] = (lanes == comb_ref[rows, :1]).astype(BF16)

    choose(0, n_front)
    head.wait()

    @pl.loop(0, dim // 256)
    def _(s):
        cols = pl.ds(pl.multiple_of(s * 256, 128), 256)
        out_ref[:, cols] = jnp.dot(sel[...], front[:, cols], preferred_element_type=F32) * scale

    @pl.loop(0, n_batch)
    def _(b):
        slot = lax.rem(b, 2)

        @pl.when(b + 1 < n_batch)
        def _():
            start(b + 1)

        choose(n_front + b * (batch * 8), batch * 8)

        @pl.loop(0, in_batch(b))
        def _(i):
            copy(0, slot, i).wait()

        @pl.loop(0, dim // 256)
        def _(s):
            cols = pl.ds(pl.multiple_of(s * 256, 128), 256)
            out_ref[:, cols] += jnp.dot(sel[:, : batch * 8], buf[slot, :, cols], preferred_element_type=F32) * scale


def gather_rows(table, local_ids, owned):
    n, dim = local_ids.shape[0], table.shape[1]
    batch, n_front = 64, 1024
    far = owned & (local_ids >= n_front)
    before = (jnp.arange(n)[:, None] > jnp.arange(n)[None]) & far[None]
    rank = jnp.sum(before.astype(I32), axis=1)
    count = jnp.sum(far.astype(I32)).reshape(1)
    comb = jnp.where(far, n_front + rank * 8 + (local_ids & 7), jnp.where(owned, local_ids, -1))
    hit = (jnp.arange(n)[:, None] == rank[None]) & far[None]
    blk = jnp.max(jnp.where(hit, (local_ids >> 3)[None], 0), axis=1)
    return pl.pallas_call(
        functools.partial(gather_kernel, batch),
        out_shape=jax.ShapeDtypeStruct((n, dim), F32),
        in_specs=[pl.BlockSpec(memory_space=pltpu.SMEM), pl.BlockSpec(memory_space=pltpu.SMEM),
                  pl.BlockSpec(memory_space=VMEM), pl.BlockSpec(memory_space=ANY)],
        out_specs=pl.BlockSpec(memory_space=VMEM),
        scratch_shapes=[
            VMEM((n_front, dim), BF16),
            VMEM((2, batch * 8, dim), BF16),
            VMEM((n, n_front), BF16),
            pltpu.SemaphoreType.DMA,
            pltpu.SemaphoreType.DMA((2,)),
        ],
        compiler_params=pltpu.CompilerParams(vmem_limit_bytes=48 * 2**20),
        name="gather_rows",
    )(blk, count, comb.reshape(n, 1), table)


class Line:
    def __init__(self, n_tp):
        self.me = lax.axis_index("tp")
        n_chip = n_tp // 2
        chip, core = lax.div(self.me, 2), lax.rem(self.me, 2)
        self.core = core
        self.partner = chip * 2 + 1 - core
        self.left, self.right, self.opp = (
            lax.rem(chip + k, n_chip) * 2 + core for k in (n_chip - 1, 1, n_chip // 2))
        self.chips = {"opp": self.opp, "right": self.right, "left": self.left, "own": self.me}

    def other(self, tp):
        return tp + 1 - 2 * self.core


def tp_copy(src, dst, sems, at, tp):
    send, recv = sems
    return pltpu.make_async_remote_copy(
        src_ref=src, dst_ref=dst, send_sem=send.at[at], recv_sem=recv.at[at],
        device_id={"tp": tp}, device_id_type=MESH)


def greet(devices):
    barrier = pltpu.get_barrier_semaphore()
    for device in devices:
        pl.semaphore_signal(barrier, inc=1, device_id=device, device_id_type=MESH)
    return barrier


def rows_kernel(n_dp, n_tp, part_ref, send_ref, w_ref, dyn_ref, dyr_ref,
                x_ref, y_ref, g_ref, wpart_ref, idx_ref,
                chip_sum, half_in, full_in, d_send, d_recv, h_send, h_recv, f_send, f_recv, i_send, i_recv):
    me = lax.axis_index("dp")
    line = Line(n_tp)
    n_pos, dim = x_ref.shape
    half = n_pos // 2
    piece = 16
    n_piece = half // piece
    order = ("opp", "right", "left", "own")

    barrier = greet([{"tp": t} for t in (line.partner, line.left, line.right)]
                    + [{"dp": lax.rem(me + i, n_dp)} for i in range(1, n_dp)])
    pl.semaphore_wait(barrier, n_dp + 2)

    def block(tp):
        return pl.ds(pl.multiple_of(tp * n_pos, n_pos), n_pos)

    def to_partner(k):
        return tp_copy(part_ref.at[block(line.other(line.chips[order[k]])), :], chip_sum.at[k],
                       (d_send, d_recv), k, line.partner)

    for k in range(4):
        to_partner(k).start()

    def idx_copy(i, to, slot):
        return pltpu.make_async_remote_copy(
            src_ref=send_ref.at[to], dst_ref=idx_ref.at[slot], send_sem=i_send.at[i], recv_sem=i_recv.at[i],
            device_id={"dp": to}, device_id_type=MESH)

    for i in range(1, n_dp):
        idx_copy(i, lax.rem(me + i, n_dp), me).start()

    def add_chip(k):
        to_partner(k).wait_recv()
        chip_sum[k] += part_ref[block(line.chips[order[k]]), :]

    def half_copy(side, q):
        rows = pl.ds(side * half + q * piece, piece)
        return tp_copy(chip_sum.at[0, rows, :], half_in.at[side, pl.ds(q * piece, piece), :],
                       (h_send, h_recv), (side, q), (line.right, line.left)[side])

    def full_copy(side, q):
        rows = pl.ds(q * piece, piece)
        return tp_copy(chip_sum.at[1 + side, rows, :], full_in.at[side, rows, :],
                       (f_send, f_recv), (side, q), (line.right, line.left)[side])

    add_chip(0)
    for q in range(n_piece):
        for side in range(2):
            half_copy(side, q).start()
    add_chip(1)
    add_chip(2)
    for q in range(n_piece):
        full_copy(0, n_piece + q).start()
        full_copy(1, q).start()
    for q in range(n_piece):
        for side in range(2):
            half_copy(side, q).wait_recv()
            rows = pl.ds(side * half + q * piece, piece)
            chip_sum[1 + side, rows, :] += half_in[side, pl.ds(q * piece, piece), :]
            full_copy(side, side * n_piece + q).start()
    add_chip(3)

    idx_ref[pl.ds(me, 1)] = send_ref[pl.ds(me, 1)]
    for i in range(1, n_dp):
        to, frm = lax.rem(me + i, n_dp), lax.rem(me + n_dp - i, n_dp)
        idx_copy(i, to, me).wait_send()
        idx_copy(i, frm, frm).wait_recv()

    gain = 1.0 + w_ref[...]
    w_acc = jnp.zeros((8, dim), F32)
    for q in list(range(n_piece)) + list(range(n_piece, 2 * n_piece)):
        for side in range(2):
            full_copy(side, q).wait_recv()
        for r in range(q * piece, (q + 1) * piece, 8):
            rows = pl.ds(r, 8)
            total = (chip_sum[3, rows, :] + full_in[0, rows, :]) + full_in[1, rows, :]
            x_emb = total.astype(BF16)
            x_ref[rows, :] = x_emb
            x = x_emb.astype(F32)
            r_inv = lax.rsqrt(jnp.mean(x * x, axis=-1, keepdims=True) + NORM_EPS)
            x_hat = x * r_inv
            y_ref[rows, :] = (x_hat * gain).astype(BF16)
            dy = dyn_ref[rows, :].astype(F32)
            a = dy * gain
            g_ref[rows, :] = dyr_ref[rows, :].astype(F32) + r_inv * (a - x_hat * jnp.mean(a * x_hat, axis=-1, keepdims=True))
            w_acc = w_acc + dy * x_hat
    wpart_ref[...] = jnp.sum(w_acc, axis=0, keepdims=True)

    for k in range(4):
        to_partner(k).wait_send()
    for q in range(n_piece):
        for side in range(2):
            half_copy(side, q).wait_send()
    for q in range(2 * n_piece):
        for side in range(2):
            full_copy(side, q).wait_send()


def rows_and_norm(n_dp, n_tp, part, send_idx, w_norm, dy_norm, dy_resid):
    n_pos, dim = dy_norm.shape
    dma = pltpu.SemaphoreType.DMA
    vmem = pl.BlockSpec(memory_space=VMEM)
    pieces = n_pos // 16
    return pl.pallas_call(
        functools.partial(rows_kernel, n_dp, n_tp),
        out_shape=(jax.ShapeDtypeStruct((n_pos, dim), BF16), jax.ShapeDtypeStruct((n_pos, dim), BF16),
                   jax.ShapeDtypeStruct((n_pos, dim), F32), jax.ShapeDtypeStruct((1, dim), F32),
                   jax.ShapeDtypeStruct(send_idx.shape, I32)),
        in_specs=[vmem] * 5,
        out_specs=(vmem,) * 5,
        scratch_shapes=[
            VMEM((4, n_pos, dim), F32),
            VMEM((2, n_pos // 2, dim), F32),
            VMEM((2, n_pos, dim), F32),
            dma((4,)), dma((4,)), dma((2, pieces // 2)), dma((2, pieces // 2)),
            dma((2, pieces)), dma((2, pieces)), dma((n_dp,)), dma((n_dp,)),
        ],
        compiler_params=pltpu.CompilerParams(collective_id=1, has_side_effects=True, vmem_limit_bytes=60 * 2**20),
        name="rows_and_norm",
    )(part, send_idx, w_norm.reshape(1, dim), dy_norm, dy_resid)


def split3(x):
    hi = x.astype(BF16)
    rest = x - hi.astype(F32)
    mid = rest.astype(BF16)
    return hi, mid, (rest - mid.astype(F32)).astype(BF16)


def dot_exact(one_hot, x):
    parts = [jnp.dot(one_hot, p, preferred_element_type=F32) for p in split3(x)]
    return (parts[2] + parts[1]) + parts[0]


NCHUNK = 9


def grad_kernel(n_dp, n_tp, slot_ref, idx_ref, g_ref, w_ref, out_ref, wout_ref,
                g_all, pick, place, send, recv, hot_send, hot_recv, w_dp, w_sum, w_tp,
                ag_send, ag_recv, send_sem, recv_sem, hot_out, hot_in, wd_send, wd_recv, wt_send, wt_recv):
    me, plane = lax.axis_index("dp"), lax.axis_index("tp")
    line = Line(n_tp)
    n_pos, dim = g_ref.shape
    n_tok = n_pos * n_tp
    wide = dim // NCHUNK
    n_slots = n_dp * STRIDE
    scale = math.sqrt(dim)
    sizes = (8, 24, 32, 40, 56)
    per = n_tp // 2
    owner = lax.div(plane, per)
    own = jnp.logical_and(plane == 0, me == owner)
    gathers_hot = jnp.logical_and(plane == 0, me < 2)

    barrier = greet([{"tp": lax.rem(plane + i, n_tp)} for i in range(1, n_tp)]
                    + [{"dp": lax.rem(me + i, n_dp)} for i in range(1, n_dp)])

    @pl.when(jnp.logical_not(own))
    def _():
        pl.semaphore_signal(barrier, inc=1, device_id={"dp": owner, "tp": 0}, device_id_type=MESH)

    @pl.when(gathers_hot)
    def _():
        @pl.loop(0, per * n_dp)
        def _(k):
            dp, tp = lax.rem(k, n_dp), lax.div(k, n_dp) + me * per

            @pl.when(jnp.logical_not(jnp.logical_and(tp == 0, dp == me)))
            def _():
                pl.semaphore_signal(barrier, inc=1, device_id={"dp": dp, "tp": tp}, device_id_type=MESH)

    extra = jnp.where(own, 0, 1) + jnp.where(gathers_hot, per * n_dp - jnp.where(own, 1, 0), 0)
    pl.semaphore_wait(barrier, n_dp + n_tp - 2 + extra)

    def n_rows(blk):
        return HOT_ROWS + cold_cap(plane, blk)

    def peer(i):
        return lax.rem(me + i, n_dp), lax.rem(me + n_dp - i, n_dp)

    def cols_of(c):
        return pl.ds(pl.multiple_of(c * wide, 128), wide)

    def block(tp, start=0, size=n_pos):
        return pl.ds(pl.multiple_of(tp * n_pos + start, 8), size)

    half = n_pos // 2
    KINDS = range(8)

    def ag_sent(kind, c):
        cols = cols_of(c)
        rows, to = (
            (block(plane), line.right), (block(plane), line.left),
            (block(line.left, 0, half), line.right), (block(line.right, half, half), line.left),
            (block(plane), line.partner), (block(line.left), line.partner),
            (block(line.right), line.partner), (block(line.opp), line.partner))[kind]
        src = g_ref.at[:, cols] if kind in (0, 1, 4) else g_all.at[rows, cols]
        return tp_copy(src, g_all.at[rows, cols], (ag_send, ag_recv), (kind, c), to)

    def ag_arrives(kind, c):
        cols = cols_of(c)
        rows = (block(line.left), block(line.right),
                block(line.opp, 0, half), block(line.opp, half, half),
                block(line.partner), block(line.other(line.left)),
                block(line.other(line.right)), block(line.other(line.opp)))[kind]
        return tp_copy(g_all.at[rows, cols], g_all.at[rows, cols], (ag_send, ag_recv), (kind, c), line.partner)

    def w_copy(i, slot):
        return pltpu.make_async_remote_copy(
            src_ref=w_ref, dst_ref=w_dp.at[slot], send_sem=wd_send.at[i], recv_sem=wd_recv.at[i],
            device_id={"dp": peer(i)[0]}, device_id_type=MESH)

    def row_copy(c, i, size, to, slot):
        return pltpu.make_async_remote_copy(
            src_ref=send.at[pl.ds(pl.multiple_of(to * STRIDE, 8), size), cols_of(c)],
            dst_ref=recv.at[slot, pl.ds(0, size), cols_of(c)],
            send_sem=send_sem.at[c, i], recv_sem=recv_sem.at[c, i],
            device_id={"dp": to}, device_id_type=MESH)

    def by_size(want, fn):
        for size in sizes:
            @pl.when(want == size)
            def _():
                fn(size)

    def setup():
        for i in range(1, n_dp):
            w_copy(i, me).start()
        g_all[block(plane), :] = g_ref[...]

        @pl.loop(0, n_slots // 128)
        def _(b):
            base = pl.multiple_of(b * 128, 128)
            rows = lax.broadcasted_iota(I32, (128, n_tok), 0) + base
            pick[pl.ds(base, 128), :] = (rows == slot_ref[...]).astype(BF16)

        @pl.loop(0, n_dp)
        def _(s):
            @pl.loop(lax.div(n_rows(me), 8), STRIDE // 8)
            def _(r):
                recv[s, pl.ds(pl.multiple_of(r * 8, 8), 8), :] = jnp.zeros((8, dim), F32)

        @pl.loop(0, n_dp // 2)
        def _(p):
            lane = lax.broadcasted_iota(I32, (1, 128), 1)
            idx = jnp.where(lane < STRIDE, idx_ref[2 * p, 0:1, :], idx_ref[2 * p + 1, 0:1, :])
            rows = lax.broadcasted_iota(I32, (place.shape[0], 128), 0)
            place[:, pl.ds(pl.multiple_of(p * 128, 128), 128)] = (rows == idx).astype(BF16)

    @pl.loop(0, NCHUNK + 3)
    def _(i):
        @pl.when(i < NCHUNK)
        def _():
            for kind in (0, 1, 4):
                ag_sent(kind, i).start()

        @pl.when(i == 0)
        def _():
            setup()

        @pl.when(jnp.logical_and(i >= 1, i < NCHUNK + 1))
        def _():
            c = i - 1
            ag_arrives(0, c).wait_recv()
            ag_sent(2, c).start()
            ag_sent(5, c).start()
            ag_arrives(1, c).wait_recv()
            ag_sent(3, c).start()
            ag_sent(6, c).start()

        @pl.when(jnp.logical_and(i >= 2, i < NCHUNK + 2))
        def _():
            c = i - 2
            ag_arrives(2, c).wait_recv()
            ag_arrives(3, c).wait_recv()
            ag_sent(7, c).start()

        @pl.when(i >= 3)
        def _():
            c = i - 3
            for kind in (4, 5, 6, 7):
                ag_arrives(kind, c).wait_recv()
            cols = cols_of(c)
            send[:, cols] = dot_exact(pick[...], g_all[:, cols])

            @pl.loop(1, n_dp)
            def _(k):
                to = peer(k)[0]
                by_size(n_rows(to), lambda size: row_copy(c, k, size, to, me).start())

    recv[pl.ds(me, 1)] = send[pl.ds(pl.multiple_of(me * STRIDE, 8), STRIDE), :][None]

    w_dp[pl.ds(me, 1)] = w_ref[...][None]
    for i in range(1, n_dp):
        w_copy(i, me).wait_send()
        w_copy(i, peer(i)[1]).wait_recv()
    w_sum[...] = jnp.sum(w_dp[...], axis=0)

    def wt_copy(i, slot):
        return tp_copy(w_sum, w_tp.at[slot], (wt_send, wt_recv), i, lax.rem(plane + i, n_tp))

    for i in range(1, n_tp):
        wt_copy(i, plane).start()
    w_tp[pl.ds(plane, 1)] = w_sum[...][None]

    @pl.loop(0, NCHUNK)
    def _(c):
        for kind in KINDS:
            ag_sent(kind, c).wait_send()

    at = pl.multiple_of(lax.rem(plane, per) * (n_dp * HOT_ROWS) + me * HOT_ROWS, 8)

    def hot_copy(c):
        return pltpu.make_async_remote_copy(
            src_ref=hot_send.at[:, cols_of(c)], dst_ref=hot_recv.at[pl.ds(at, HOT_ROWS), cols_of(c)],
            send_sem=hot_out.at[c], recv_sem=hot_in.at[0],
            device_id={"dp": owner, "tp": 0}, device_id_type=MESH)

    @pl.loop(0, NCHUNK)
    def _(c):
        @pl.loop(1, n_dp)
        def _(i):
            to, frm = peer(i)
            by_size(n_rows(to), lambda size: row_copy(c, i, size, to, me).wait_send())
            by_size(n_rows(me), lambda size: row_copy(c, i, size, frm, frm).wait_recv())

        cols = cols_of(c)
        rows = recv[:, :, cols]
        hot_send[:, cols] = jnp.sum(rows[:, :HOT_ROWS, :], axis=0) * scale

        @pl.when(jnp.logical_not(own))
        def _():
            hot_copy(c).start()

        out_ref[:, cols] = dot_exact(place[...], rows.reshape(n_slots, wide)) * scale

    for i in range(1, n_tp):
        wt_copy(i, plane).wait_send()
        wt_copy(i, lax.rem(plane + n_tp - i, n_tp)).wait_recv()
    wout_ref[...] = jnp.sum(w_tp[...], axis=0)

    @pl.when(jnp.logical_not(own))
    def _():
        @pl.loop(0, NCHUNK)
        def _(c):
            hot_copy(c).wait_send()

    def hot_wait(n):
        ref = hot_recv.at[pl.ds(0, n), :]
        pltpu.make_async_remote_copy(
            src_ref=ref, dst_ref=ref, send_sem=hot_out.at[0], recv_sem=hot_in.at[0],
            device_id={"dp": 1, "tp": 0}, device_id_type=MESH).wait_recv()

    total = hot_recv.shape[0]

    @pl.when(own)
    def _():
        hot_recv[0:HOT_ROWS, :] = hot_send[...]
        hot_wait(total - HOT_ROWS)

    @pl.when(jnp.logical_and(plane == 0, me == 1))
    def _():
        hot_wait(total)

    @pl.when(gathers_hot)
    def _():
        out_ref[...] += hot_recv[...]


def exchange_grads(n_dp, n_tp, out_rows, slot, idx, g, w_part):
    n_pos, dim = g.shape
    n_tok = n_pos * n_tp
    dma = pltpu.SemaphoreType.DMA
    vmem = pl.BlockSpec(memory_space=VMEM)
    return pl.pallas_call(
        functools.partial(grad_kernel, n_dp, n_tp),
        out_shape=(jax.ShapeDtypeStruct((out_rows, dim), F32), jax.ShapeDtypeStruct(w_part.shape, F32)),
        in_specs=[vmem] * 4,
        out_specs=(vmem,) * 2,
        scratch_shapes=[
            VMEM((n_tok, dim), F32),
            VMEM((n_dp * STRIDE, n_tok), BF16),
            VMEM((out_rows, n_dp * STRIDE), BF16),
            VMEM((n_dp * STRIDE, dim), F32),
            VMEM((n_dp, STRIDE, dim), F32),
            VMEM((HOT_ROWS, dim), F32),
            VMEM((HOT // 2, dim), F32),
            VMEM((n_dp,) + w_part.shape, F32),
            VMEM(w_part.shape, F32),
            VMEM((n_tp,) + w_part.shape, F32),
            dma((8, NCHUNK)), dma((8, NCHUNK)),
            dma((NCHUNK, n_dp)), dma((NCHUNK, n_dp)), dma((NCHUNK,)), dma((1,)),
            dma((n_dp,)), dma((n_dp,)), dma((n_tp,)), dma((n_tp,)),
        ],
        compiler_params=pltpu.CompilerParams(collective_id=2, has_side_effects=True, vmem_limit_bytes=62 * 2**20),
        name="exchange_grads",
    )(slot, idx, g, w_part)


def swap(x, axis):
    return lax.all_to_all(x, axis, split_axis=0, concat_axis=0)


def dense_grads(n_dp, n_tp, out_rows, tokens, g, w_part):
    g_all = swap(jnp.broadcast_to(g, (n_tp,) + g.shape), "tp").reshape(-1, g.shape[1])
    rows = n_dp * out_rows
    local = tokens - lax.axis_index("tp") * rows
    drop = jnp.where((local >= 0) & (local < rows), local, rows)
    shard = jax.ops.segment_sum(g_all, drop, num_segments=rows, mode="drop")
    emb = jnp.sum(swap(shard.reshape(n_dp, out_rows, -1), "dp"), axis=0) * math.sqrt(g_all.shape[1])
    w = jnp.sum(swap(jnp.broadcast_to(w_part, (n_dp,) + w_part.shape), "dp"), axis=0)
    w = jnp.sum(swap(jnp.broadcast_to(w, (n_tp,) + w.shape), "tp"), axis=0)
    return emb, w


def route(n_dp, n_tp, out_rows, ids):
    plane = lax.axis_index("tp")
    n = ids.shape[0]
    cold = ids >= HOT
    bins = ids // out_rows
    hits = (bins[:, None] == jnp.arange(n_dp * n_tp)[None]) & cold[:, None]
    bin_no = jnp.arange(n_dp * n_tp)
    flag = jnp.any(jnp.sum(hits.astype(I32), axis=0) > cold_cap(bin_no // n_dp, bin_no % n_dp))
    blk = bins % n_dp
    mine = cold & (bins // n_dp == plane)
    block_hit = (blk[:, None] == jnp.arange(n_dp)[None]) & mine[:, None]
    before = (jnp.arange(n)[:, None] > jnp.arange(n)[None]).astype(BF16)
    rank = jnp.sum(jnp.where(block_hit, jnp.dot(before, block_hit.astype(BF16), preferred_element_type=F32), 0.0), axis=1).astype(I32)
    cold_slot = blk * STRIDE + HOT_ROWS + rank
    per_plane = HOT // n_tp
    in_plane = ids % per_plane
    hot_slot = (in_plane // HOT_ROWS) * STRIDE + in_plane % HOT_ROWS
    hot = jnp.logical_not(cold) & (ids // per_plane == plane)
    slot = jnp.where(mine, cold_slot, jnp.where(hot, hot_slot, -1))
    slots = jnp.arange(n_dp * STRIDE)
    row = jnp.max(jnp.where((slots[:, None] == slot[None]) & mine[None], (ids % out_rows)[None], -1), axis=1)
    row = row.reshape(n_dp, 1, STRIDE)
    row = jnp.concatenate([row, row], axis=2)
    send = jnp.where(jnp.arange(8)[None, :, None] == 1, flag.astype(I32), row)
    return slot.reshape(1, n), send


def solution(mesh):
    n_dp, n_tp = mesh.shape["dp"], mesh.shape["tp"]

    def local_step(tokens, emb_table, w_norm, dy_norm, dy_resid):
        shard_rows, dim = emb_table.shape
        out_rows = shard_rows // n_dp
        ids = tokens[0]
        slot, send_idx = route(n_dp, n_tp, out_rows, ids)
        local_ids = ids - lax.axis_index("tp") * shard_rows
        owned = (local_ids >= 0) & (local_ids < shard_rows)
        part = gather_rows(emb_table, local_ids, owned)
        x_emb, y_norm, g, w_part, idx = rows_and_norm(n_dp, n_tp, part, send_idx, w_norm, dy_norm[0], dy_resid[0])
        fits = jnp.max(idx[:, 1, :]) == 0
        emb_grad, w_sum = lax.cond(
            fits,
            lambda: exchange_grads(n_dp, n_tp, out_rows, slot, idx, g, w_part),
            lambda: dense_grads(n_dp, n_tp, out_rows, ids, g, w_part),
        )
        return x_emb[None], y_norm[None], emb_grad, w_sum[0]

    act_spec = P("dp", "tp", None)
    return jax.shard_map(local_step, mesh=mesh, in_specs=(P("dp", None), P("tp", None), P(None), act_spec, act_spec), out_specs=(act_spec, act_spec, P(("tp", "dp"), None), P(None)), check_vma=False)
```

time: 319 us -> 195 us (0.61); the launches traced: 314 us -> 194 us
  waiting for transfers between devices: 120 us -> 0 us
  between operations: 15.5 us -> 2.09 us
  Pallas kernels: 162 us -> 173 us
    reduce_scatter x1 -> x0, waiting for transfers between devices: 87.8 us -> none  [local_step(): lax.psum_scatter(partial_rows, 'tp', scatter_dimension=1, tiled=True)]
    all_gather x1 -> x0, waiting for transfers between devices: 32.4 us -> none  [local_step(): g_all = lax.all_gather(tok_grad, 'tp', axis=1, tiled=True)[0]]
    pallas_call x2, Pallas kernels: 63 us -> 79.1 us  [the longest x1 49.4 us: rows_and_norm(): pl.pallas_call(functools.partial(rows_kernel, n_dp, n_tp), out_shape=(jax...]
    pallas_call x1, Pallas kernels: 99.2 us -> 93.8 us  [exchange_grads(): pl.pallas_call(functools.partial(grad_kernel, n_dp, n_tp), out_shape=(jax...]
    unnamed x13 -> x15, local copies, waits for them, and re-layouts: 5.45 us -> 7.59 us
  transfers between devices with their start and end apart: 2 -> 0, of which waited for: 2 -> 0; matrix products, arithmetic and copies ran while one was open for 1% -> 0% of each run, Pallas kernels for 5% -> 0%
where the time goes in v2:
time: 195 us; the launch traced here: 194 us
  Pallas kernels  173 us (89%)
  other arithmetic  9.26 us (5%)
  local copies, waits for them, and re-layouts  8.7 us (4%)
  between operations  2.09 us (1%)
    pallas_call x1, Pallas kernels, exchange_grads(): pl.pallas_call(functools.partial(grad_kernel, n_dp, n_tp), out_shape=(jax...  93.8 us
    pallas_call x1, Pallas kernels, rows_and_norm(): pl.pallas_call(functools.partial(rows_kernel, n_dp, n_tp), out_shape=(jax...  49.4 us
    pallas_call x1, Pallas kernels, gather_rows(): pl.pallas_call(functools.partial(gather_kernel, batch), out_shape=jax.Sha...  29.7 us
    unnamed x15, local copies, waits for them, and re-layouts  7.59 us

profile of v2, /device:TPU:0, one launch (start us, length us, event | category | flops | bytes accessed | tf_op | source)
XLA Modules:
  0.0 193.7 jit_solution(14529746516720396489)
XLA Ops:
  0.6 0.8 fusion.23
  1.4 0.7 fusion.20
  2.1 0.5 fusion.5
  2.7 0.8 fusion.17
  3.4 0.0 copy-start.2
  3.5 0.2 convert_reduce_fusion
  3.7 2.1 %select_reduce_fusion = (s32[1024]{0:T(1024)S(1)}, s32[1024]{0:T(1024)S(1)}) fusion(s32[1024]{0:T(1024)S(1)} %bitcast.27, s32[1024]{0:T(1024)S(1)} %bitcast.25, pred[1024]{0:T(1024)(128)(4,1)S(1)} %get-tuple-element.44, s32[1024]{0:T(1024)S(1)} %bitcast.28, pred[1024]{0:T(1024)(128)(4,1)S(1)} %get-tuple-element.54, s32[1024]{0:T(1024)S(1)} %convert_reduce_fusion), kind=kLoop, calls=%fused_computation.3 | loop fusion | flops 8386560 | bytes 26624 | tf_op jit(solution)/shard_map/reduce_max | solution.py:586
  5.8 1.3 convert_reduce_fusion.2
  7.1 0.0 copy-done.2
  7.1 0.2 copy.23
  7.4 0.2 copy.27
  7.6 0.1 select_select_fusion.comb_ref
  7.7 0.0 copy-start.4
  7.8 29.7 %gather_rows.1.part_ref = f32[1024,2304]{1,0:T(8,128)} custom-call(s32[1024]{0:T(1024)S(1)} %get-tuple-element.56.blk_ref, s32[1]{0:T(128)} %bitcast.4.count_ref, s32[1024,1]{1,0:T(8,128)S(1)} %select_select_fusion.comb_ref, bf16[8192,2304]{1,0:T(8,128)(2,1)} %table_ref.1), custom_call_target="tpu_custom_call" | custom-call | tf_op jit(solution)/shard_map/gather_rows/pallas_call | solution.py:103
  37.5 0.1 reshape.182
  37.5 0.1 add_bitcast_fusion
  37.6 0.4 convert_reduce_fusion.1
  38.0 0.6 compare_reduce_fusion
  39.3 0.7 broadcast_select_fusion.send_ref
  40.0 0.0 copy-done.4
  40.0 0.6 reshape.183.w_ref
  40.6 49.4 %rows_and_norm.1 = (bf16[128,2304]{1,0:T(8,128)(2,1)}, bf16[128,2304]{1,0:T(8,128)(2,1)}, f32[128,2304]{1,0:T(8,128)S(1)}, f32[1,2304]{1,0:T(1,128)S(1)}, s32[16,8,128]{2,1,0:T(8,128)S(1)}) custom-call(f32[1024,2304]{1,0:T(8,128)} %gather_rows.1.part_ref, s32[16,8,128]{2,1,0:T(8,128)} %broadcast_select_fusion.send_ref, f32[1,2304]{1,0:T(1,128)} %reshape.183.w_ref, ...), custom_call_target="tpu_custom_call" | custom-call | tf_op jit(solution)/shard_map/rows_and_norm/pallas_call | solution.py:255
  90.0 0.6 slice_reduce_fusion
  91.3 0.0 copy-done.1
  91.3 0.0 copy-done.3
  91.4 94.7 %conditional.1 = (f32[512,2304]{1,0:T(8,128)}, f32[2304]{0:T(1024)S(1)}) conditional(s32[]{:T(128)} %convert_element_type.36, (s32[1024]{0:T(1024)S(1)}, f32[128,2304]{1,0:T(8,128)S(1)}, f32[1,2304]{1,0:T(1,128)S(1)}) %tuple.34, (s32[1,1024]{1,0:T(1,128)S(1)}, s32[16,8,128]{2,1,0:T(8,128)S(1)}, f32[128,2304]{1,0:T(8,128)S(1)}, ...), branch_computations={%region_8.13_spmd, %region_13.14_spmd} | conditional | flops 21289476 | bytes 459909248 | solution.py:606
  91.6 93.8 %exchange_grads.1 = (f32[512,2304]{1,0:T(8,128)}, f32[1,2304]{1,0:T(1,128)}) custom-call(s32[1,1024]{1,0:T(1,128)S(1)} %get-tuple-element.20.slot_ref, s32[16,8,128]{2,1,0:T(8,128)S(1)} %get-tuple-element.21.idx_ref, f32[128,2304]{1,0:T(8,128)S(1)} %get-tuple-element.22.g_ref, f32[1,2304]{1,0:T(1,128)S(1)} %get-tuple-element.23.w_ref), custom_call_target="tpu_custom_call" | custom-call | tf_op jit(solution)/shard_map/cond/branch_1_fun/exchange_grads/pallas_call | solution.py:525
  185.4 0.7 reduce.3
  186.1 0.0 copy-start.5
  186.1 1.9 copy.39
  188.0 0.8 copy.40
  188.8 4.8 %copy.41 = f32[512,2304]{1,0:T(8,128)} copy(f32[512,2304]{1,0:T(8,128)} %get-tuple-element.67) | data formatting | bytes 9437184
  (10 shorter events, 0.0 us)
Async XLA Ops:
  3.4 3.7 %copy-start.2 = (s32[1,1024]{1,0:T(1,128)}, s32[1,1024]{1,0:T(1,128)S(1)}, u32[]{:S(2)}) copy-start(s32[1,1024]{1,0:T(1,128)S(1)} %get-tuple-element.51) | copy-start | bytes 12292
  7.7 32.2 %copy-start.4 = (f32[2304]{0:T(1024)S(1)}, f32[2304]{0:T(1024)}, u32[]{:S(2)}) copy-start(f32[2304]{0:T(1024)} %param.9) | copy-start | bytes 27652
  40.6 50.7 %copy-start.1 = (s32[1,1024]{1,0:T(1,128)S(1)}, s32[1,1024]{1,0:T(1,128)}, u32[]{:S(2)}) copy-start(s32[1,1024]{1,0:T(1,128)} %param.7) | copy-start | bytes 12292
  40.6 50.7 %copy-start.3 = (s32[1,1024]{1,0:T(1,128)S(1)}, s32[1,1024]{1,0:T(1,128)}, u32[]{:S(2)}) copy-start(s32[1,1024]{1,0:T(1,128)} %copy-done.2) | copy-start | bytes 12292
  91.3 96.7 %copy-start = (bf16[128,2304]{1,0:T(8,128)(2,1)S(1)}, bf16[128,2304]{1,0:T(8,128)(2,1)}, u32[]{:S(2)}) copy-start(bf16[128,2304]{1,0:T(8,128)(2,1)} %get-tuple-element.38) | copy-start | bytes 1769476
  186.1 7.6 %copy-start.5 = (f32[2304]{0:T(1024)}, f32[2304]{0:T(1024)S(1)}, u32[]{:S(2)}) copy-start(f32[2304]{0:T(1024)S(1)} %get-tuple-element.68) | copy-start | bytes 27652

commit v3 on v0

v3 whole, which is shorter than its diff:
```python
import functools
import math
import jax
import jax.numpy as jnp
from jax import lax
from jax.experimental import pallas as pl
from jax.experimental.pallas import tpu as pltpu
from jax.sharding import PartitionSpec as P

NORM_EPS = 1e-6
MESH = pl.DeviceIdType.MESH
HOT = 1024
STRIDE = 64
HOT_ROWS = 8
F32 = jnp.float32
BF16 = jnp.bfloat16
I32 = jnp.int32
VMEM = pltpu.VMEM
ANY = pl.ANY


def cold_cap(tp, blk):
    first = jnp.where(blk < 2, 0, jnp.where(blk < 4, 48, jnp.where(blk < 8, 32, 24)))
    return jnp.where(tp == 0, first, 16)


def gather_kernel(batch, blk_ref, count_ref, comb_ref, front_ref, table_ref, out_ref, near, far, sel, sel2, sems):
    n_front, wide = front_ref.shape
    n_tok = out_ref.shape[0]
    scale = math.sqrt(table_ref.shape[1])
    count = count_ref[0]
    n_batch = lax.div(count + batch - 1, batch)
    step = pl.program_id(0)

    def pair(b, i):
        return pl.ds(pl.multiple_of(blk_ref[b * batch + i] * 2, 2), 2), pl.ds(pl.multiple_of(i * 2, 2), 2)

    def near_copy(i):
        src, dst = pair(0, i)
        return pltpu.make_async_copy(table_ref.at[src, :], near.at[dst, :], sems.at[0])

    def choose(ref, base):
        @pl.loop(0, n_tok // 128)
        def _(r):
            rows = pl.ds(pl.multiple_of(r * 128, 128), 128)
            lanes = lax.broadcasted_iota(I32, (128, ref.shape[1]), 1) + base
            ref[rows, :] = (lanes == comb_ref[rows, :1]).astype(BF16)

    first = jnp.minimum(count, batch)

    @pl.when(step == 0)
    def _():
        near[...] = jnp.zeros(near.shape, BF16)

        @pl.loop(0, first)
        def _(i):
            near_copy(i).start()

        choose(sel, 0)

    out_ref[...] = jnp.dot(sel[:, :n_front], front_ref[...], preferred_element_type=F32) * scale

    @pl.when(step == 0)
    def _():
        @pl.loop(0, first)
        def _(i):
            near_copy(0).wait()

    cols = pl.ds(pl.multiple_of(step * wide, 128), wide)
    out_ref[...] += jnp.dot(sel[:, n_front:], near[:, cols], preferred_element_type=F32) * scale

    @pl.loop(1, n_batch)
    def _(b):
        here = jnp.minimum(count - b * batch, batch)

        def far_copy(i):
            src, dst = pair(b, i)
            return pltpu.make_async_copy(table_ref.at[src, cols], far.at[dst, :], sems.at[1])

        far[...] = jnp.zeros(far.shape, BF16)

        @pl.loop(0, here)
        def _(i):
            far_copy(i).start()

        choose(sel2, n_front + b * (2 * batch))

        @pl.loop(0, here)
        def _(i):
            far_copy(0).wait()

        out_ref[...] += jnp.dot(sel2[...], far[...], preferred_element_type=F32) * scale


def gather_rows(table, local_ids, owned):
    n, dim = local_ids.shape[0], table.shape[1]
    batch, n_front, wide = 320, 512, 256
    far = owned & (local_ids >= n_front)
    before = (jnp.arange(n)[:, None] > jnp.arange(n)[None]) & far[None]
    rank = jnp.sum(before.astype(I32), axis=1)
    count = jnp.sum(far.astype(I32)).reshape(1)
    comb = jnp.where(far, n_front + rank * 2 + (local_ids & 1), jnp.where(owned, local_ids, -1))
    hit = (jnp.arange(n)[:, None] == rank[None]) & far[None]
    blk = jnp.max(jnp.where(hit, (local_ids >> 1)[None], 0), axis=1)
    blk = jnp.pad(blk, (0, -n % batch))
    return pl.pallas_call(
        functools.partial(gather_kernel, batch),
        out_shape=jax.ShapeDtypeStruct((n, dim), F32),
        grid_spec=pltpu.PrefetchScalarGridSpec(
            num_scalar_prefetch=2,
            grid=(dim // wide,),
            in_specs=[pl.BlockSpec((n, 1), lambda i, *_: (0, 0)),
                      pl.BlockSpec((n_front, wide), lambda i, *_: (0, i)),
                      pl.BlockSpec(memory_space=ANY)],
            out_specs=pl.BlockSpec((n, wide), lambda i, *_: (0, i)),
            scratch_shapes=[
                VMEM((2 * batch, dim), BF16),
                VMEM((2 * batch, wide), BF16),
                VMEM((n, n_front + 2 * batch), BF16),
                VMEM((n, 2 * batch), BF16),
                pltpu.SemaphoreType.DMA((2,)),
            ],
        ),
        compiler_params=pltpu.CompilerParams(dimension_semantics=("arbitrary",), vmem_limit_bytes=32 * 2**20),
        name="gather_rows",
    )(blk, count, comb.reshape(n, 1), table, table)


class Line:
    def __init__(self, n_tp):
        self.me = lax.axis_index("tp")
        n_chip = n_tp // 2
        chip, core = lax.div(self.me, 2), lax.rem(self.me, 2)
        self.core = core
        self.partner = chip * 2 + 1 - core
        self.left, self.right, self.opp = (
            lax.rem(chip + k, n_chip) * 2 + core for k in (n_chip - 1, 1, n_chip // 2))
        self.chips = {"opp": self.opp, "right": self.right, "left": self.left, "own": self.me}

    def other(self, tp):
        return tp + 1 - 2 * self.core


def tp_copy(src, dst, sems, at, tp):
    send, recv = sems
    return pltpu.make_async_remote_copy(
        src_ref=src, dst_ref=dst, send_sem=send.at[at], recv_sem=recv.at[at],
        device_id={"tp": tp}, device_id_type=MESH)


def greet(devices):
    barrier = pltpu.get_barrier_semaphore()
    for device in devices:
        pl.semaphore_signal(barrier, inc=1, device_id=device, device_id_type=MESH)
    return barrier


def split3(x):
    hi = x.astype(BF16)
    rest = x - hi.astype(F32)
    mid = rest.astype(BF16)
    return hi, mid, (rest - mid.astype(F32)).astype(BF16)


def dot_exact(one_hot, x):
    parts = [jnp.dot(one_hot, p, preferred_element_type=F32) for p in split3(x)]
    return (parts[2] + parts[1]) + parts[0]


NCHUNK = 9
LAG = 4
PIECE = 16


def step_kernel(n_dp, n_tp, part_ref, slot_ref, send_ref, gain_ref, dyn_ref, dyr_ref,
                x_ref, y_ref, g_ref, out_ref, wout_ref, idx_ref,
                mine, chip_sum, half_in, full_in, g_all, pick, place, send, recv, hot_send, hot_recv,
                w_part, w_dp, w_sum, w_tp,
                m_sem, d_send, d_recv, h_send, h_recv, f_send, f_recv, i_send, i_recv,
                ag_send, ag_recv, a_send, a_recv, hot_out, hot_in, wd_send, wd_recv, wt_send, wt_recv):
    me, plane = lax.axis_index("dp"), lax.axis_index("tp")
    line = Line(n_tp)
    n_pos, dim = x_ref.shape
    half = n_pos // 2
    n_tok = n_pos * n_tp
    wide = dim // NCHUNK
    n_slots = n_dp * STRIDE
    n_piece = half // PIECE
    scale = math.sqrt(dim)
    sizes = (8, 24, 32, 40, 56)
    order = ("opp", "right", "left", "own")
    per = n_tp // 2
    owner = lax.div(plane, per)
    own = jnp.logical_and(plane == 0, me == owner)
    gathers_hot = jnp.logical_and(plane == 0, me < 2)

    def block(tp, start=0, size=n_pos):
        return pl.ds(pl.multiple_of(tp * n_pos + start, 8), size)

    def mine_copy(k):
        return pltpu.make_async_copy(part_ref.at[block(line.chips[order[k]]), :], mine.at[k], m_sem.at[k])

    for k in range(4):
        mine_copy(k).start()

    barrier = greet([{"tp": lax.rem(plane + i, n_tp)} for i in range(1, n_tp)]
                    + [{"dp": lax.rem(me + i, n_dp)} for i in range(1, n_dp)])

    @pl.when(jnp.logical_not(own))
    def _():
        pl.semaphore_signal(barrier, inc=1, device_id={"dp": owner, "tp": 0}, device_id_type=MESH)

    @pl.when(gathers_hot)
    def _():
        @pl.loop(0, per * n_dp)
        def _(k):
            dp, tp = lax.rem(k, n_dp), lax.div(k, n_dp) + me * per

            @pl.when(jnp.logical_not(jnp.logical_and(tp == 0, dp == me)))
            def _():
                pl.semaphore_signal(barrier, inc=1, device_id={"dp": dp, "tp": tp}, device_id_type=MESH)

    extra = jnp.where(own, 0, 1) + jnp.where(gathers_hot, per * n_dp - jnp.where(own, 1, 0), 0)
    pl.semaphore_wait(barrier, n_dp + n_tp - 2 + extra)

    def peer(i):
        return lax.rem(me + i, n_dp), lax.rem(me + n_dp - i, n_dp)

    def to_partner(k):
        return tp_copy(part_ref.at[block(line.other(line.chips[order[k]])), :], chip_sum.at[k],
                       (d_send, d_recv), k, line.partner)

    for k in range(4):
        to_partner(k).start()

    def idx_copy(i, to, slot):
        return pltpu.make_async_remote_copy(
            src_ref=send_ref.at[to], dst_ref=idx_ref.at[slot], send_sem=i_send.at[i], recv_sem=i_recv.at[i],
            device_id={"dp": to}, device_id_type=MESH)

    for i in range(1, n_dp):
        idx_copy(i, peer(i)[0], me).start()

    def add_chip(k):
        mine_copy(k).wait()
        to_partner(k).wait_recv()
        chip_sum[k] += mine[k]

    def half_copy(side, q):
        rows = pl.ds(side * half + q * PIECE, PIECE)
        return tp_copy(chip_sum.at[0, rows, :], half_in.at[side, pl.ds(q * PIECE, PIECE), :],
                       (h_send, h_recv), (side, q), (line.right, line.left)[side])

    def full_copy(side, q):
        rows = pl.ds(q * PIECE, PIECE)
        return tp_copy(chip_sum.at[1 + side, rows, :], full_in.at[side, rows, :],
                       (f_send, f_recv), (side, q), (line.right, line.left)[side])

    add_chip(0)
    for q in range(n_piece):
        for side in range(2):
            half_copy(side, q).start()
    add_chip(1)
    add_chip(2)
    for q in range(n_piece):
        full_copy(0, n_piece + q).start()
        full_copy(1, q).start()

    def n_rows(blk):
        return HOT_ROWS + cold_cap(plane, blk)

    for q in range(n_piece):
        for side in range(2):
            half_copy(side, q).wait_recv()
            rows = pl.ds(side * half + q * PIECE, PIECE)
            chip_sum[1 + side, rows, :] += half_in[side, pl.ds(q * PIECE, PIECE), :]
            full_copy(side, side * n_piece + q).start()
    add_chip(3)

    @pl.loop(0, n_slots // 128)
    def _(b):
        base = pl.multiple_of(b * 128, 128)
        rows = lax.broadcasted_iota(I32, (128, n_tok), 0) + base
        pick[pl.ds(base, 128), :] = (rows == slot_ref[...]).astype(BF16)

    @pl.loop(0, n_dp)
    def _(s):
        @pl.loop(lax.div(n_rows(me), 8), STRIDE // 8)
        def _(r):
            recv[s, pl.ds(pl.multiple_of(r * 8, 8), 8), :] = jnp.zeros((8, dim), F32)

    idx_ref[pl.ds(me, 1)] = send_ref[pl.ds(me, 1)]
    for i in range(1, n_dp):
        to, frm = peer(i)
        idx_copy(i, to, me).wait_send()
        idx_copy(i, frm, frm).wait_recv()

    @pl.loop(0, n_dp // 2)
    def _(p):
        lane = lax.broadcasted_iota(I32, (1, 128), 1)
        idx = jnp.where(lane < STRIDE, idx_ref[2 * p, 0:1, :], idx_ref[2 * p + 1, 0:1, :])
        rows = lax.broadcasted_iota(I32, (place.shape[0], 128), 0)
        place[:, pl.ds(pl.multiple_of(p * 128, 128), 128)] = (rows == idx).astype(BF16)

    gain = 1.0 + gain_ref[...]
    w_acc = jnp.zeros((8, dim), F32)
    for q in range(2 * n_piece):
        for side in range(2):
            full_copy(side, q).wait_recv()
        for r in range(q * PIECE, (q + 1) * PIECE, 8):
            rows = pl.ds(r, 8)
            total = (chip_sum[3, rows, :] + full_in[0, rows, :]) + full_in[1, rows, :]
            x_emb = total.astype(BF16)
            x_ref[rows, :] = x_emb
            x = x_emb.astype(F32)
            r_inv = lax.rsqrt(jnp.mean(x * x, axis=-1, keepdims=True) + NORM_EPS)
            x_hat = x * r_inv
            y_ref[rows, :] = (x_hat * gain).astype(BF16)
            dy = dyn_ref[rows, :].astype(F32)
            a = dy * gain
            g_ref[rows, :] = dyr_ref[rows, :].astype(F32) + r_inv * (a - x_hat * jnp.mean(a * x_hat, axis=-1, keepdims=True))
            w_acc = w_acc + dy * x_hat
    w_part[...] = jnp.sum(w_acc, axis=0, keepdims=True)

    def cols_of(c):
        return pl.ds(pl.multiple_of(c * wide, 128), wide)

    def ag_sent(kind, c):
        cols = cols_of(c)
        rows, to = (
            (block(plane), line.right), (block(plane), line.left),
            (block(line.left, 0, half), line.right), (block(line.right, half, half), line.left),
            (block(plane), line.partner), (block(line.left), line.partner),
            (block(line.right), line.partner), (block(line.opp), line.partner))[kind]
        src = g_ref.at[:, cols] if kind in (0, 1, 4) else g_all.at[rows, cols]
        return tp_copy(src, g_all.at[rows, cols], (ag_send, ag_recv), (kind, c), to)

    def ag_arrives(kind, c):
        cols = cols_of(c)
        rows = (block(line.left), block(line.right),
                block(line.opp, 0, half), block(line.opp, half, half),
                block(line.partner), block(line.other(line.left)),
                block(line.other(line.right)), block(line.other(line.opp)))[kind]
        return tp_copy(g_all.at[rows, cols], g_all.at[rows, cols], (ag_send, ag_recv), (kind, c), line.partner)

    def w_copy(i, slot):
        return pltpu.make_async_remote_copy(
            src_ref=w_part, dst_ref=w_dp.at[slot], send_sem=wd_send.at[i], recv_sem=wd_recv.at[i],
            device_id={"dp": peer(i)[0]}, device_id_type=MESH)

    def wt_copy(i, slot):
        return tp_copy(w_sum, w_tp.at[slot], (wt_send, wt_recv), i, lax.rem(plane + i, n_tp))

    def row_copy(c, i, size, to, slot):
        return pltpu.make_async_remote_copy(
            src_ref=send.at[pl.ds(pl.multiple_of(to * STRIDE, 8), size), cols_of(c)],
            dst_ref=recv.at[slot, pl.ds(0, size), cols_of(c)],
            send_sem=a_send.at[c, i], recv_sem=a_recv.at[c, i],
            device_id={"dp": to}, device_id_type=MESH)

    def by_size(want, fn):
        for size in sizes:
            @pl.when(want == size)
            def _():
                fn(size)

    at = pl.multiple_of(lax.rem(plane, per) * (n_dp * HOT_ROWS) + me * HOT_ROWS, 8)

    def hot_copy(c):
        return pltpu.make_async_remote_copy(
            src_ref=hot_send.at[:, cols_of(c)], dst_ref=hot_recv.at[pl.ds(at, HOT_ROWS), cols_of(c)],
            send_sem=hot_out.at[c], recv_sem=hot_in.at[0],
            device_id={"dp": owner, "tp": 0}, device_id_type=MESH)

    def send_own(c):
        for kind in (0, 1, 4):
            ag_sent(kind, c).start()

    send_own(0)
    send_own(1)
    for i in range(1, n_dp):
        w_copy(i, me).start()
    g_all[block(plane), :] = g_ref[...]

    @pl.loop(0, NCHUNK + 2 + LAG)
    def _(i):
        @pl.when(i + 2 < NCHUNK)
        def _():
            send_own(i + 2)

        @pl.when(i < NCHUNK)
        def _():
            ag_arrives(0, i).wait_recv()
            ag_sent(2, i).start()
            ag_sent(5, i).start()
            ag_arrives(1, i).wait_recv()
            ag_sent(3, i).start()
            ag_sent(6, i).start()

        @pl.when(jnp.logical_and(i >= 1, i < NCHUNK + 1))
        def _():
            ag_arrives(2, i - 1).wait_recv()
            ag_arrives(3, i - 1).wait_recv()
            ag_sent(7, i - 1).start()

        @pl.when(jnp.logical_and(i >= 2, i < NCHUNK + 2))
        def _():
            c = i - 2
            for kind in (4, 5, 6, 7):
                ag_arrives(kind, c).wait_recv()
            cols = cols_of(c)
            send[:, cols] = dot_exact(pick[...], g_all[:, cols])

            @pl.loop(1, n_dp)
            def _(k):
                to = peer(k)[0]
                by_size(n_rows(to), lambda size: row_copy(c, k, size, to, me).start())

            recv[pl.ds(me, 1), :, cols] = send[pl.ds(pl.multiple_of(me * STRIDE, 8), STRIDE), cols][None]

        @pl.when(i == 3)
        def _():
            w_dp[pl.ds(me, 1)] = w_part[...][None]
            for k in range(1, n_dp):
                w_copy(k, me).wait_send()
                w_copy(k, peer(k)[1]).wait_recv()
            w_sum[...] = jnp.sum(w_dp[...], axis=0)
            for k in range(1, n_tp):
                wt_copy(k, plane).start()
            w_tp[pl.ds(plane, 1)] = w_sum[...][None]

        @pl.when(i >= 2 + LAG)
        def _():
            c = i - 2 - LAG

            @pl.loop(1, n_dp)
            def _(k):
                to, frm = peer(k)
                by_size(n_rows(to), lambda size: row_copy(c, k, size, to, me).wait_send())
                by_size(n_rows(me), lambda size: row_copy(c, k, size, frm, frm).wait_recv())

            cols = cols_of(c)
            rows = recv[:, :, cols]
            hot_send[:, cols] = jnp.sum(rows[:, :HOT_ROWS, :], axis=0) * scale

            @pl.when(jnp.logical_not(own))
            def _():
                hot_copy(c).start()

            out_ref[:, cols] = dot_exact(place[...], rows.reshape(n_slots, wide)) * scale

    for i in range(1, n_tp):
        wt_copy(i, plane).wait_send()
        wt_copy(i, lax.rem(plane + n_tp - i, n_tp)).wait_recv()
    wout_ref[...] = jnp.sum(w_tp[...], axis=0)

    for k in range(4):
        to_partner(k).wait_send()
    for q in range(n_piece):
        for side in range(2):
            half_copy(side, q).wait_send()
    for q in range(2 * n_piece):
        for side in range(2):
            full_copy(side, q).wait_send()

    @pl.loop(0, NCHUNK)
    def _(c):
        for kind in range(8):
            ag_sent(kind, c).wait_send()

    @pl.when(jnp.logical_not(own))
    def _():
        @pl.loop(0, NCHUNK)
        def _(c):
            hot_copy(c).wait_send()

    def hot_wait(n):
        ref = hot_recv.at[pl.ds(0, n), :]
        pltpu.make_async_remote_copy(
            src_ref=ref, dst_ref=ref, send_sem=hot_out.at[0], recv_sem=hot_in.at[0],
            device_id={"dp": 1, "tp": 0}, device_id_type=MESH).wait_recv()

    total = hot_recv.shape[0]

    @pl.when(own)
    def _():
        hot_recv[0:HOT_ROWS, :] = hot_send[...]
        hot_wait(total - HOT_ROWS)

    @pl.when(jnp.logical_and(plane == 0, me == 1))
    def _():
        hot_wait(total)

    @pl.when(gathers_hot)
    def _():
        out_ref[...] += hot_recv[...]


def fused_step(n_dp, n_tp, out_rows, part, slot, send_idx, w_norm, dy_norm, dy_resid):
    n_pos, dim = dy_norm.shape
    n_tok = n_pos * n_tp
    half, pieces = n_pos // 2, n_pos // PIECE
    dma = pltpu.SemaphoreType.DMA
    vmem = pl.BlockSpec(memory_space=VMEM)
    shape = jax.ShapeDtypeStruct
    return pl.pallas_call(
        functools.partial(step_kernel, n_dp, n_tp),
        out_shape=(shape((n_pos, dim), BF16), shape((n_pos, dim), BF16), shape((n_pos, dim), F32),
                   shape((out_rows, dim), F32), shape((1, dim), F32), shape(send_idx.shape, I32)),
        in_specs=[pl.BlockSpec(memory_space=ANY)] + [vmem] * 5,
        out_specs=(vmem,) * 6,
        scratch_shapes=[
            VMEM((4, n_pos, dim), F32),
            VMEM((4, n_pos, dim), F32),
            VMEM((2, half, dim), F32),
            VMEM((2, n_pos, dim), F32),
            VMEM((n_tok, dim), F32),
            VMEM((n_dp * STRIDE, n_tok), BF16),
            VMEM((out_rows, n_dp * STRIDE), BF16),
            VMEM((n_dp * STRIDE, dim), F32),
            VMEM((n_dp, STRIDE, dim), F32),
            VMEM((HOT_ROWS, dim), F32),
            VMEM((HOT // 2, dim), F32),
            VMEM((1, dim), F32),
            VMEM((n_dp, 1, dim), F32),
            VMEM((1, dim), F32),
            VMEM((n_tp, 1, dim), F32),
            dma((4,)), dma((4,)), dma((4,)), dma((2, pieces // 2)), dma((2, pieces // 2)),
            dma((2, pieces)), dma((2, pieces)), dma((n_dp,)), dma((n_dp,)),
            dma((8, NCHUNK)), dma((8, NCHUNK)),
            dma((NCHUNK, n_dp)), dma((NCHUNK, n_dp)), dma((NCHUNK,)), dma((1,)),
            dma((n_dp,)), dma((n_dp,)), dma((n_tp,)), dma((n_tp,)),
        ],
        compiler_params=pltpu.CompilerParams(collective_id=1, has_side_effects=True, vmem_limit_bytes=67043328),
        name="fused_step",
    )(part, slot, send_idx, w_norm.reshape(1, dim), dy_norm, dy_resid)


def swap(x, axis):
    return lax.all_to_all(x, axis, split_axis=0, concat_axis=0)


def dense_grads(n_dp, n_tp, out_rows, tokens, g):
    g_all = swap(jnp.broadcast_to(g, (n_tp,) + g.shape), "tp").reshape(-1, g.shape[1])
    rows = n_dp * out_rows
    local = tokens - lax.axis_index("tp") * rows
    drop = jnp.where((local >= 0) & (local < rows), local, rows)
    shard = jax.ops.segment_sum(g_all, drop, num_segments=rows, mode="drop")
    return jnp.sum(swap(shard.reshape(n_dp, out_rows, -1), "dp"), axis=0) * math.sqrt(g.shape[1])


def route(n_dp, n_tp, out_rows, ids):
    plane = lax.axis_index("tp")
    n = ids.shape[0]
    cold = ids >= HOT
    bins = ids // out_rows
    hits = (bins[:, None] == jnp.arange(n_dp * n_tp)[None]) & cold[:, None]
    bin_no = jnp.arange(n_dp * n_tp)
    flag = jnp.any(jnp.sum(hits.astype(I32), axis=0) > cold_cap(bin_no // n_dp, bin_no % n_dp))
    blk = bins % n_dp
    mine = cold & (bins // n_dp == plane)
    block_hit = (blk[:, None] == jnp.arange(n_dp)[None]) & mine[:, None]
    before = (jnp.arange(n)[:, None] > jnp.arange(n)[None]).astype(BF16)
    rank = jnp.sum(jnp.where(block_hit, jnp.dot(before, block_hit.astype(BF16), preferred_element_type=F32), 0.0), axis=1).astype(I32)
    cold_slot = blk * STRIDE + HOT_ROWS + rank
    per_plane = HOT // n_tp
    in_plane = ids % per_plane
    hot_slot = (in_plane // HOT_ROWS) * STRIDE + in_plane % HOT_ROWS
    hot = jnp.logical_not(cold) & (ids // per_plane == plane)
    slot = jnp.where(mine, cold_slot, jnp.where(hot, hot_slot, -1))
    slots = jnp.arange(n_dp * STRIDE)
    row = jnp.max(jnp.where((slots[:, None] == slot[None]) & mine[None], (ids % out_rows)[None], -1), axis=1)
    row = row.reshape(n_dp, 1, STRIDE)
    row = jnp.concatenate([row, row], axis=2)
    send = jnp.where(jnp.arange(8)[None, :, None] == 1, flag.astype(I32), row)
    return slot.reshape(1, n), send


def solution(mesh):
    n_dp, n_tp = mesh.shape["dp"], mesh.shape["tp"]

    def local_step(tokens, emb_table, w_norm, dy_norm, dy_resid):
        shard_rows, dim = emb_table.shape
        out_rows = shard_rows // n_dp
        ids = tokens[0]
        slot, send_idx = route(n_dp, n_tp, out_rows, ids)
        local_ids = ids - lax.axis_index("tp") * shard_rows
        owned = (local_ids >= 0) & (local_ids < shard_rows)
        part = gather_rows(emb_table, local_ids, owned)
        x_emb, y_norm, g, emb_fast, w_sum, idx = fused_step(
            n_dp, n_tp, out_rows, part, slot, send_idx, w_norm, dy_norm[0], dy_resid[0])
        fits = jnp.max(idx[:, 1, :]) == 0
        emb_grad = lax.cond(fits, lambda: emb_fast, lambda: dense_grads(n_dp, n_tp, out_rows, ids, g))
        return x_emb[None], y_norm[None], emb_grad, w_sum[0]

    act_spec = P("dp", "tp", None)
    return jax.shard_map(local_step, mesh=mesh, in_specs=(P("dp", None), P("tp", None), P(None), act_spec, act_spec), out_specs=(act_spec, act_spec, P(("tp", "dp"), None), P(None)), check_vma=False)
```

time: 881 us -> 188 us (0.21)
  waiting for transfers between devices: 468 us -> 0 us
  other arithmetic: 260 us -> 9.99 us
  Pallas kernels: 0 us -> 162 us
  blocking collectives: 71.9 us -> 0 us
  local copies, waits for them, and re-layouts: 63.5 us -> 12.6 us
  between operations: 13.8 us -> 2.09 us
    reduce_scatter x2 -> x0, waiting for transfers between devices: 414 us -> none  [the longest x1 337 us: local_step(): lax.psum_scatter(shard_grad, 'dp', scatter_dimension=0, tiled=True)]
    scatter-add x1 -> x0, other arithmetic: 199 us -> none  [local_step(): jax.ops.segment_sum(seq_grad.reshape(-1, model_dim), drop_ids.reshape(-1)...]
    pallas_call x0 -> x2, Pallas kernels: none -> 162 us  [the longest x1 141 us: fused_step(): pl.pallas_call(functools.partial(step_kernel, n_dp, n_tp), out_shape=(sha...]
    psum x1 -> x0, blocking collectives: 71.9 us -> none  [local_step(): w_grad = lax.psum(jnp.sum(dy_float * x_hat, axis=(0, 1)), ('dp', 'tp'))]
    all_gather x1 -> x0, waiting for transfers between devices: 53.7 us -> none  [local_step(): seq_grad = lax.all_gather(tok_grad, 'tp', axis=1, tiled=True)]
    mul x1 -> x0, other arithmetic: 49.9 us -> none  [local_step(): jax.ops.segment_sum(seq_grad.reshape(-1, model_dim), drop_ids.reshape(-1)...]
    gather x1 -> x0, local copies, waits for them, and re-layouts: 39 us -> none  [local_step(): looked_up = jnp.take(emb_table, jnp.where(owned_mask, local_ids, 0), axis=0)]
    broadcast_in_dim x1 -> x0, local copies, waits for them, and re-layouts: 23.8 us -> none  [local_step(): jax.ops.segment_sum(seq_grad.reshape(-1, model_dim), drop_ids.reshape(-1)...]
  transfers between devices with their start and end apart: 3 -> 0, of which waited for: 3 -> 0; matrix products, arithmetic and copies ran while one was open for 0% -> 0% of each run, Pallas kernels for 0% -> 0%
where the time goes in v3:
time: 188 us
  Pallas kernels  162 us (86%)
  local copies, waits for them, and re-layouts  12.6 us (7%)
  other arithmetic  9.99 us (5%)
  between operations  2.09 us (1%)
    pallas_call x1, Pallas kernels, fused_step(): pl.pallas_call(functools.partial(step_kernel, n_dp, n_tp), out_shape=(sha...  141 us
    pallas_call x1, Pallas kernels, gather_rows(): pl.pallas_call(functools.partial(gather_kernel, batch), out_shape=jax.Sha...  21.1 us
    unnamed x13, local copies, waits for them, and re-layouts  10.7 us

profile of v3, /device:TPU:0, one launch (start us, length us, event | category | flops | bytes accessed | tf_op | source)
XLA Modules:
  0.0 187.5 jit_solution(17554536669143673496)
XLA Ops:
  0.6 1.3 convert_reduce_fusion.2
  2.0 0.7 fusion.20
  2.7 0.3 convert_reduce_fusion.1
  3.0 0.6 compare_reduce_fusion
  4.3 0.5 fusion.5
  4.8 1.3 reshape.175.gain_ref
  6.2 0.8 fusion.23
  6.9 0.2 convert_reduce_fusion
  7.2 0.8 fusion.17
  8.0 0.0 copy-start.4
  8.0 2.1 %select_reduce_fusion = (s32[1024]{0:T(1024)S(1)}, s32[1024]{0:T(1024)S(1)}) fusion(s32[1024]{0:T(1024)S(1)} %bitcast.27, s32[1024]{0:T(1024)S(1)} %bitcast.25, pred[1024]{0:T(1024)(128)(4,1)S(1)} %get-tuple-element.26, s32[1024]{0:T(1024)S(1)} %bitcast.28, pred[1024]{0:T(1024)(128)(4,1)S(1)} %get-tuple-element.36, s32[1024]{0:T(1024)S(1)} %convert_reduce_fusion), kind=kLoop, calls=%fused_computation.3 | loop fusion | flops 8386560 | bytes 26624 | tf_op jit(solution)/shard_map/reduce_max | solution.py:572
  10.1 0.0 copy-done.4
  10.1 0.1 reshape.174
  10.2 0.1 add_bitcast_fusion
  10.3 0.7 broadcast_select_fusion.send_ref
  11.0 0.2 copy.19
  11.2 0.2 copy.15
  11.4 0.1 select_select_fusion.comb_ref
  11.6 21.1 %gather_rows.1.part_ref = f32[1024,2304]{1,0:T(8,128)S(1)} custom-call(s32[1280]{0:T(1024)S(1)} %pad.4.blk_ref, s32[1]{0:T(128)} %bitcast.4.count_ref, s32[1024,1]{1,0:T(8,128)S(1)} %select_select_fusion.comb_ref, bf16[8192,2304]{1,0:T(8,128)(2,1)} %table_ref.1, bf16[8192,2304]{1,0:T(8,128)(2,1)} %table_ref.1), custom_call_target="tpu_custom_call" | custom-call | tf_op jit(solution)/shard_map/gather_rows/pallas_call | solution.py:106
  32.7 0.0 copy-start
  32.7 3.6 %copy-done = f32[1024,2304]{1,0:T(8,128)} copy-done((f32[1024,2304]{1,0:T(8,128)}, f32[1024,2304]{1,0:T(8,128)S(1)}, u32[]{:S(2)}) %copy-start) | copy-done | bytes 9437208
  36.3 141.3 %fused_step.1 = (bf16[128,2304]{1,0:T(8,128)(2,1)}, bf16[128,2304]{1,0:T(8,128)(2,1)}, f32[128,2304]{1,0:T(8,128)}, f32[512,2304]{1,0:T(8,128)}, f32[1,2304]{1,0:T(1,128)}, /*index=5*/s32[16,8,128]{2,1,0:T(8,128)}) custom-call(f32[1024,2304]{1,0:T(8,128)} %copy-done, s32[1,1024]{1,0:T(1,128)} %copy-done.4, s32[16,8,128]{2,1,0:T(8,128)} %broadcast_select_fusion.send_ref, ...), custom_call_target="tpu_custom_call" | custom-call | tf_op jit(solution)/shard_map/fused_step/pallas_call | solution.py:506
  177.6 1.5 slice_reduce_fusion
  179.7 0.0 copy-start.5
  179.7 0.0 copy-start.2
  179.7 0.0 copy-start.1
  179.8 0.7 copy-done.5
  180.4 0.6 reduce.3
  181.1 0.0 copy-done.2
  181.1 0.8 copy.27
  181.9 0.8 copy.28
  182.7 4.8 %copy.29 = f32[512,2304]{1,0:T(8,128)} copy(f32[512,2304]{1,0:T(8,128)} %get-tuple-element.47) | data formatting | bytes 9437184
  (8 shorter events, 0.0 us)
Async XLA Ops:
  8.0 2.1 %copy-start.4 = (s32[1,1024]{1,0:T(1,128)}, s32[1,1024]{1,0:T(1,128)S(1)}, u32[]{:S(2)}) copy-start(s32[1,1024]{1,0:T(1,128)S(1)} %get-tuple-element.33.slot_ref) | copy-start | bytes 12292
  32.7 3.6 %copy-start = (f32[1024,2304]{1,0:T(8,128)}, f32[1024,2304]{1,0:T(8,128)S(1)}, u32[]{:S(2)}) copy-start(f32[1024,2304]{1,0:T(8,128)S(1)} %gather_rows.1.part_ref) | copy-start | bytes 28311556
  179.7 0.7 copy-start.5
  179.7 1.3 copy-start.2
  179.7 2.1 %copy-start.1 = (bf16[128,2304]{1,0:T(8,128)(2,1)S(1)}, bf16[128,2304]{1,0:T(8,128)(2,1)}, u32[]{:S(2)}) copy-start(bf16[128,2304]{1,0:T(8,128)(2,1)} %get-tuple-element.21) | copy-start | bytes 1769476

commit v4 on v3

v4 whole, which is shorter than its diff:
```python
import functools
import math
import jax
import jax.numpy as jnp
from jax import lax
from jax.experimental import pallas as pl
from jax.experimental.pallas import tpu as pltpu
from jax.sharding import PartitionSpec as P

NORM_EPS = 1e-6
MESH = pl.DeviceIdType.MESH
HOT = 768
HOT_PLANE = 2
HOT_ROWS = 8
STRIDE = 64
SLOTS = 512
FRONT = 512
FAR = 320
NCHUNK = 9
LAG = 3
F32 = jnp.float32
BF16 = jnp.bfloat16
I32 = jnp.int32
VMEM = pltpu.VMEM
ANY = pl.ANY


def hot_rows(tp):
    return jnp.where(tp >= HOT_PLANE, HOT_ROWS, 0)


def cold_cap(tp, blk):
    first = jnp.where(blk == 0, 0, jnp.where(blk == 1, 40, jnp.where(blk < 4, 48, jnp.where(blk < 8, 32, 24))))
    return jnp.where(tp == 0, first, 16)


def slot_base(tp, blk):
    first = jnp.where(blk < 2, 0, jnp.where(blk < 4, 40 + 48 * (blk - 2), jnp.where(blk < 8, 136 + 32 * (blk - 4), 264 + 24 * (blk - 8))))
    return jnp.where(tp == 0, first, (16 + hot_rows(tp)) * blk)


def far_kernel(blk_ref, count_ref, table_ref, out_ref, sem):
    count = jnp.minimum(count_ref[0], FAR)
    out_ref[...] = jnp.zeros(out_ref.shape, BF16)

    def copy(i):
        return pltpu.make_async_copy(
            table_ref.at[pl.ds(pl.multiple_of(blk_ref[i] * 2, 2), 2), :],
            out_ref.at[pl.ds(pl.multiple_of(i * 2, 2), 2), :], sem)

    @pl.loop(0, count)
    def _(i):
        copy(i).start()

    @pl.loop(0, count)
    def _(i):
        copy(0).wait()


def far_rows(table, blk, count):
    return pl.pallas_call(
        far_kernel,
        out_shape=jax.ShapeDtypeStruct((2 * FAR, table.shape[1]), BF16),
        in_specs=[pl.BlockSpec(memory_space=pltpu.SMEM), pl.BlockSpec(memory_space=pltpu.SMEM),
                  pl.BlockSpec(memory_space=ANY)],
        out_specs=pl.BlockSpec(memory_space=VMEM),
        scratch_shapes=[pltpu.SemaphoreType.DMA],
        compiler_params=pltpu.CompilerParams(vmem_limit_bytes=16 * 2**20),
        name="far_rows",
    )(blk, count, table)


class Line:
    def __init__(self, n_tp):
        self.me = lax.axis_index("tp")
        n_chip = n_tp // 2
        chip, core = lax.div(self.me, 2), lax.rem(self.me, 2)
        self.core = core
        self.partner = chip * 2 + 1 - core
        self.left, self.right, self.opp = (
            lax.rem(chip + k, n_chip) * 2 + core for k in (n_chip - 1, 1, n_chip // 2))
        self.chips = {"opp": self.opp, "right": self.right, "left": self.left, "own": self.me}

    def other(self, tp):
        return tp + 1 - 2 * self.core


def tp_copy(src, dst, sems, at, tp):
    send, recv = sems
    return pltpu.make_async_remote_copy(
        src_ref=src, dst_ref=dst, send_sem=send.at[at], recv_sem=recv.at[at],
        device_id={"tp": tp}, device_id_type=MESH)


def greet(devices):
    barrier = pltpu.get_barrier_semaphore()
    for device in devices:
        pl.semaphore_signal(barrier, inc=1, device_id=device, device_id_type=MESH)
    return barrier


def split3(x):
    hi = x.astype(BF16)
    rest = x - hi.astype(F32)
    mid = rest.astype(BF16)
    return hi, mid, (rest - mid.astype(F32)).astype(BF16)


def dot_exact(one_hot, x):
    parts = [jnp.dot(one_hot, p, preferred_element_type=F32) for p in split3(x)]
    return (parts[2] + parts[1]) + parts[0]


def step_kernel(n_dp, n_tp, comb_ref, far_ref, front_ref, slot_ref, send_ref, gain_ref, dyn_ref, dyr_ref,
                x_ref, y_ref, out_ref, wout_ref, idx_ref,
                sel, mine, chip_sum, half_in, full_in, g_ref, g_all, pick, place, send, recv, hot_send, hot_recv,
                w_acc, w_part, w_dp, w_sum, w_tp,
                d_send, d_recv, h_send, h_recv, f_send, f_recv, i_send, i_recv,
                ag_send, ag_recv, a_send, a_recv, hot_out, hot_in, wd_send, wd_recv, wt_send, wt_recv):
    me, plane = lax.axis_index("dp"), lax.axis_index("tp")
    line = Line(n_tp)
    n_pos, dim = x_ref.shape
    half = n_pos // 2
    n_tok = n_pos * n_tp
    wide = dim // NCHUNK
    n_slots = n_dp * STRIDE
    scale = math.sqrt(dim)
    sizes = (16, 24, 32, 40, 48)
    order = ("opp", "right", "left", "own")
    per = out_ref.shape[0] // (n_dp * HOT_ROWS)
    is_hot = plane >= HOT_PLANE
    owner = lax.div(jnp.maximum(plane - HOT_PLANE, 0), per)
    gathers_hot = jnp.logical_and(plane == 0, me < 2)
    n_sources = jnp.where(me == 0, n_dp * per, n_dp * (n_tp - HOT_PLANE - per))

    def block(tp, start=0, size=n_pos):
        return pl.ds(pl.multiple_of(tp * n_pos + start, 8), size)

    barrier = greet([{"tp": lax.rem(plane + i, n_tp)} for i in range(1, n_tp)]
                    + [{"dp": lax.rem(me + i, n_dp)} for i in range(1, n_dp)])

    @pl.when(is_hot)
    def _():
        pl.semaphore_signal(barrier, inc=1, device_id={"dp": owner, "tp": 0}, device_id_type=MESH)

    @pl.when(gathers_hot)
    def _():
        @pl.loop(0, n_sources)
        def _(k):
            tp = HOT_PLANE + per * me + lax.div(k, n_dp)
            pl.semaphore_signal(barrier, inc=1, device_id={"dp": lax.rem(k, n_dp), "tp": tp}, device_id_type=MESH)

    extra = jnp.where(is_hot, 1, 0) + jnp.where(gathers_hot, n_sources, 0)
    pl.semaphore_wait(barrier, n_dp + n_tp - 2 + extra)

    def peer(i):
        return lax.rem(me + i, n_dp), lax.rem(me + n_dp - i, n_dp)

    def cols_of(c):
        return pl.ds(pl.multiple_of(c * wide, 128), wide)

    def idx_copy(i, to, slot):
        return pltpu.make_async_remote_copy(
            src_ref=send_ref.at[to], dst_ref=idx_ref.at[slot], send_sem=i_send.at[i], recv_sem=i_recv.at[i],
            device_id={"dp": to}, device_id_type=MESH)

    for i in range(1, n_dp):
        idx_copy(i, peer(i)[0], me).start()

    def to_partner(k, c):
        return tp_copy(send.at[pl.ds(k * n_pos, n_pos), cols_of(c)], chip_sum.at[k, :, cols_of(c)],
                       (d_send, d_recv), (k, c), line.partner)

    def look_up(k):
        mine_tp = line.chips[order[k]]
        for part, tp in enumerate((line.other(mine_tp), mine_tp)):
            lanes = lax.broadcasted_iota(I32, (n_pos, sel.shape[1]), 1)
            sel[pl.ds(part * n_pos, n_pos), :] = (lanes == comb_ref[block(tp), :]).astype(BF16)

        @pl.loop(0, NCHUNK)
        def _(c):
            cols = cols_of(c)
            rows = jnp.dot(sel[:, :FRONT], front_ref[:, cols], preferred_element_type=F32)
            rows = (rows + jnp.dot(sel[:, FRONT:], far_ref[:, cols], preferred_element_type=F32)) * scale
            send[pl.ds(k * n_pos, n_pos), cols] = rows[:n_pos]
            mine[k, :, cols] = rows[n_pos:]
            to_partner(k, c).start()

    def add_chip(k, c):
        to_partner(k, c).wait_recv()
        chip_sum[k, :, cols_of(c)] += mine[k, :, cols_of(c)]

    def half_copy(side, c):
        return tp_copy(chip_sum.at[0, pl.ds(side * half, half), cols_of(c)], half_in.at[side, :, cols_of(c)],
                       (h_send, h_recv), (side, c), (line.right, line.left)[side])

    def full_copy(side, part, c):
        rows = pl.ds(part * half, half)
        return tp_copy(chip_sum.at[1 + side, rows, cols_of(c)], full_in.at[side, rows, cols_of(c)],
                       (f_send, f_recv), (2 * side + part, c), (line.right, line.left)[side])

    look_up(0)

    @pl.loop(0, NCHUNK)
    def _(c):
        add_chip(0, c)
        for side in range(2):
            half_copy(side, c).start()

    look_up(1)
    look_up(2)

    @pl.loop(0, NCHUNK)
    def _(c):
        add_chip(1, c)
        full_copy(0, 1, c).start()
        add_chip(2, c)
        full_copy(1, 0, c).start()

    @pl.loop(0, NCHUNK)
    def _(c):
        for side in range(2):
            half_copy(side, c).wait_recv()
            chip_sum[1 + side, pl.ds(side * half, half), cols_of(c)] += half_in[side, :, cols_of(c)]
            full_copy(side, side, c).start()

    look_up(3)

    def n_rows(blk):
        return hot_rows(plane) + cold_cap(plane, blk)

    @pl.loop(0, SLOTS // 128)
    def _(b):
        base = pl.multiple_of(b * 128, 128)
        rows = lax.broadcasted_iota(I32, (128, n_tok), 0) + base
        pick[pl.ds(base, 128), :] = (rows == slot_ref[...]).astype(BF16)

    @pl.loop(0, n_dp)
    def _(s):
        @pl.loop(lax.div(n_rows(me), 8), STRIDE // 8)
        def _(r):
            recv[s, pl.ds(pl.multiple_of(r * 8, 8), 8), :] = jnp.zeros((8, dim), F32)

    idx_ref[pl.ds(me, 1)] = send_ref[pl.ds(me, 1)]
    for i in range(1, n_dp):
        to, frm = peer(i)
        idx_copy(i, to, me).wait_send()
        idx_copy(i, frm, frm).wait_recv()

    @pl.loop(0, n_dp // 2)
    def _(p):
        lane = lax.broadcasted_iota(I32, (1, 128), 1)
        idx = jnp.where(lane < STRIDE, idx_ref[2 * p, 0:1, :], idx_ref[2 * p + 1, 0:1, :])
        rows = lax.broadcasted_iota(I32, (place.shape[0], 128), 0)
        place[:, pl.ds(pl.multiple_of(p * 128, 128), 128)] = (rows == idx).astype(BF16)

    gain = 1.0 + gain_ref[...]
    w_acc[...] = jnp.zeros(w_acc.shape, F32)

    @pl.loop(0, NCHUNK)
    def _(c):
        add_chip(3, c)
        for side in range(2):
            for part in range(2):
                full_copy(side, part, c).wait_recv()

        for k in range(4):
            to_partner(k, c).wait_send()

    @pl.loop(0, n_pos // 16)
    def _(q):
        for r in range(2):
            rows = pl.ds(pl.multiple_of(q * 16 + r * 8, 8), 8)
            total = (chip_sum[3, rows, :] + full_in[0, rows, :]) + full_in[1, rows, :]
            x_emb = total.astype(BF16)
            x_ref[rows, :] = x_emb
            x = x_emb.astype(F32)
            r_inv = lax.rsqrt(jnp.mean(x * x, axis=-1, keepdims=True) + NORM_EPS)
            x_hat = x * r_inv
            y_ref[rows, :] = (x_hat * gain).astype(BF16)
            dy = dyn_ref[rows, :].astype(F32)
            a = dy * gain
            g_ref[rows, :] = dyr_ref[rows, :].astype(F32) + r_inv * (a - x_hat * jnp.mean(a * x_hat, axis=-1, keepdims=True))
            w_acc[...] += dy * x_hat

    w_part[...] = jnp.sum(w_acc[...], axis=0, keepdims=True)

    def ag_sent(kind, c):
        cols = cols_of(c)
        rows, to = (
            (block(plane), line.right), (block(plane), line.left),
            (block(line.left, 0, half), line.right), (block(line.right, half, half), line.left),
            (block(plane), line.partner), (block(line.left), line.partner),
            (block(line.right), line.partner), (block(line.opp), line.partner))[kind]
        src = g_ref.at[:, cols] if kind in (0, 1, 4) else g_all.at[rows, cols]
        return tp_copy(src, g_all.at[rows, cols], (ag_send, ag_recv), (kind, c), to)

    def ag_arrives(kind, c):
        cols = cols_of(c)
        rows = (block(line.left), block(line.right),
                block(line.opp, 0, half), block(line.opp, half, half),
                block(line.partner), block(line.other(line.left)),
                block(line.other(line.right)), block(line.other(line.opp)))[kind]
        return tp_copy(g_all.at[rows, cols], g_all.at[rows, cols], (ag_send, ag_recv), (kind, c), line.partner)

    def w_copy(i, slot):
        return pltpu.make_async_remote_copy(
            src_ref=w_part, dst_ref=w_dp.at[slot], send_sem=wd_send.at[i], recv_sem=wd_recv.at[i],
            device_id={"dp": peer(i)[0]}, device_id_type=MESH)

    def wt_copy(i, slot):
        return tp_copy(w_sum, w_tp.at[slot], (wt_send, wt_recv), i, lax.rem(plane + i, n_tp))

    def row_copy(c, i, size, to, slot):
        return pltpu.make_async_remote_copy(
            src_ref=send.at[pl.ds(pl.multiple_of(slot_base(plane, to), 8), size), cols_of(c)],
            dst_ref=recv.at[slot, pl.ds(0, size), cols_of(c)],
            send_sem=a_send.at[c, i], recv_sem=a_recv.at[c, i],
            device_id={"dp": to}, device_id_type=MESH)

    def by_size(want, fn):
        for size in sizes:
            @pl.when(want == size)
            def _():
                fn(size)

    at = pl.multiple_of(lax.rem(jnp.maximum(plane - HOT_PLANE, 0), per) * (n_dp * HOT_ROWS) + me * HOT_ROWS, 8)

    def hot_copy(c):
        return pltpu.make_async_remote_copy(
            src_ref=hot_send.at[:, cols_of(c)], dst_ref=hot_recv.at[pl.ds(at, HOT_ROWS), cols_of(c)],
            send_sem=hot_out.at[c], recv_sem=hot_in.at[0],
            device_id={"dp": owner, "tp": 0}, device_id_type=MESH)

    def send_own(c):
        for kind in (0, 1, 4):
            ag_sent(kind, c).start()

    send_own(0)
    send_own(1)
    for i in range(1, n_dp):
        w_copy(i, me).start()
    g_all[block(plane), :] = g_ref[...]

    @pl.loop(0, NCHUNK + 2 + LAG)
    def _(i):
        @pl.when(i + 2 < NCHUNK)
        def _():
            send_own(i + 2)

        @pl.when(i < NCHUNK)
        def _():
            ag_arrives(0, i).wait_recv()
            ag_sent(2, i).start()
            ag_sent(5, i).start()
            ag_arrives(1, i).wait_recv()
            ag_sent(3, i).start()
            ag_sent(6, i).start()

        @pl.when(jnp.logical_and(i >= 1, i < NCHUNK + 1))
        def _():
            ag_arrives(2, i - 1).wait_recv()
            ag_arrives(3, i - 1).wait_recv()
            ag_sent(7, i - 1).start()

        @pl.when(jnp.logical_and(i >= 2, i < NCHUNK + 2))
        def _():
            c = i - 2
            for kind in (4, 5, 6, 7):
                ag_arrives(kind, c).wait_recv()
            cols = cols_of(c)
            send[:, cols] = dot_exact(pick[...], g_all[:, cols])

            @pl.loop(1, n_dp)
            def _(k):
                to = peer(k)[0]
                by_size(n_rows(to), lambda size: row_copy(c, k, size, to, me).start())

            def keep(size):
                recv[pl.ds(me, 1), :size, cols] = send[pl.ds(pl.multiple_of(slot_base(plane, me), 8), size), cols][None]

            by_size(n_rows(me), keep)

        @pl.when(i == 3)
        def _():
            w_dp[pl.ds(me, 1)] = w_part[...][None]
            for k in range(1, n_dp):
                w_copy(k, me).wait_send()
                w_copy(k, peer(k)[1]).wait_recv()
            w_sum[...] = jnp.sum(w_dp[...], axis=0)
            for k in range(1, n_tp):
                wt_copy(k, plane).start()
            w_tp[pl.ds(plane, 1)] = w_sum[...][None]

        @pl.when(i >= 2 + LAG)
        def _():
            c = i - 2 - LAG

            @pl.loop(1, n_dp)
            def _(k):
                to, frm = peer(k)
                by_size(n_rows(to), lambda size: row_copy(c, k, size, to, me).wait_send())
                by_size(n_rows(me), lambda size: row_copy(c, k, size, frm, frm).wait_recv())

            cols = cols_of(c)
            rows = recv[:, :, cols]

            @pl.when(is_hot)
            def _():
                hot_send[:, cols] = jnp.sum(rows[:, :HOT_ROWS, :], axis=0) * scale
                hot_copy(c).start()

            out_ref[:, cols] = dot_exact(place[...], rows.reshape(n_slots, wide)) * scale

    for i in range(1, n_tp):
        wt_copy(i, plane).wait_send()
        wt_copy(i, lax.rem(plane + n_tp - i, n_tp)).wait_recv()
    wout_ref[...] = jnp.sum(w_tp[...], axis=0)

    @pl.loop(0, NCHUNK)
    def _(c):
        for side in range(2):
            half_copy(side, c).wait_send()
            for part in range(2):
                full_copy(side, part, c).wait_send()

    @pl.loop(0, NCHUNK)
    def _(c):
        for kind in range(8):
            ag_sent(kind, c).wait_send()

    @pl.when(is_hot)
    def _():
        @pl.loop(0, NCHUNK)
        def _(c):
            hot_copy(c).wait_send()

    def take_hot(n):
        ref = hot_recv.at[pl.ds(0, n), :]
        pltpu.make_async_remote_copy(
            src_ref=ref, dst_ref=ref, send_sem=hot_out.at[0], recv_sem=hot_in.at[0],
            device_id={"dp": 2, "tp": 0}, device_id_type=MESH).wait_recv()
        out_ref[pl.ds(0, n), :] += hot_recv[pl.ds(0, n), :]

    total = hot_recv.shape[0]

    @pl.when(jnp.logical_and(plane == 0, me == 0))
    def _():
        take_hot(total)

    @pl.when(jnp.logical_and(plane == 0, me == 1))
    def _():
        take_hot(HOT - total)


def fused_step(n_dp, n_tp, out_rows, comb, far, table, slot, send_idx, w_norm, dy_norm, dy_resid):
    n_pos, dim = dy_norm.shape
    n_tok = n_pos * n_tp
    half = n_pos // 2
    dma = pltpu.SemaphoreType.DMA
    vmem = pl.BlockSpec(memory_space=VMEM)
    shape = jax.ShapeDtypeStruct
    return pl.pallas_call(
        functools.partial(step_kernel, n_dp, n_tp),
        grid=(1,),
        out_shape=(shape((n_pos, dim), BF16), shape((n_pos, dim), BF16),
                   shape((out_rows, dim), F32), shape((1, dim), F32), shape(send_idx.shape, I32)),
        in_specs=[vmem, vmem, pl.BlockSpec((FRONT, dim), lambda i: (0, 0), pipeline_mode=pl.Buffered(1))] + [vmem] * 5,
        out_specs=(vmem,) * 5,
        scratch_shapes=[
            VMEM((2 * n_pos, FRONT + 2 * FAR), BF16),
            VMEM((4, n_pos, dim), F32),
            VMEM((4, n_pos, dim), F32),
            VMEM((2, half, dim), F32),
            VMEM((2, n_pos, dim), F32),
            VMEM((n_pos, dim), F32),
            VMEM((n_tok, dim), F32),
            VMEM((SLOTS, n_tok), BF16),
            VMEM((out_rows, n_dp * STRIDE), BF16),
            VMEM((SLOTS, dim), F32),
            VMEM((n_dp, STRIDE, dim), F32),
            VMEM((HOT_ROWS, dim), F32),
            VMEM((out_rows, dim), F32),
            VMEM((8, dim), F32),
            VMEM((1, dim), F32),
            VMEM((n_dp, 1, dim), F32),
            VMEM((1, dim), F32),
            VMEM((n_tp, 1, dim), F32),
            dma((4, NCHUNK)), dma((4, NCHUNK)), dma((2, NCHUNK)), dma((2, NCHUNK)),
            dma((4, NCHUNK)), dma((4, NCHUNK)), dma((n_dp,)), dma((n_dp,)),
            dma((8, NCHUNK)), dma((8, NCHUNK)),
            dma((NCHUNK, n_dp)), dma((NCHUNK, n_dp)), dma((NCHUNK,)), dma((1,)),
            dma((n_dp,)), dma((n_dp,)), dma((n_tp,)), dma((n_tp,)),
        ],
        compiler_params=pltpu.CompilerParams(collective_id=1, has_side_effects=True, vmem_limit_bytes=67043328),
        name="fused_step",
    )(comb, far, table, slot, send_idx, w_norm.reshape(1, dim), dy_norm, dy_resid)


def swap(x, axis):
    return lax.all_to_all(x, axis, split_axis=0, concat_axis=0)


def dense_step(n_dp, n_tp, out_rows, ids, table, w_norm, dy_norm, dy_resid):
    dim = table.shape[1]
    rows = table.shape[0]
    scale = math.sqrt(dim)
    local = ids - lax.axis_index("tp") * rows
    owned = (local >= 0) & (local < rows)
    looked = jnp.take(table, jnp.where(owned, local, 0), axis=0).astype(F32) * scale
    part = jnp.where(owned[:, None], looked, 0.0).reshape((n_tp,) + dy_norm.shape)
    x_emb = jnp.sum(swap(part, "tp"), axis=0).astype(BF16)
    x = x_emb.astype(F32)
    r_inv = lax.rsqrt(jnp.mean(x * x, axis=-1, keepdims=True) + NORM_EPS)
    x_hat = x * r_inv
    gain = 1.0 + w_norm
    y_norm = (x_hat * gain).astype(BF16)
    dy = dy_norm.astype(F32)
    a = dy * gain
    g = dy_resid.astype(F32) + r_inv * (a - x_hat * jnp.mean(a * x_hat, axis=-1, keepdims=True))
    w = jnp.sum(dy * x_hat, axis=0)[None]
    w = jnp.sum(swap(jnp.broadcast_to(w, (n_dp,) + w.shape), "dp"), axis=0)
    w = jnp.sum(swap(jnp.broadcast_to(w, (n_tp,) + w.shape), "tp"), axis=0)
    g_all = swap(jnp.broadcast_to(g, (n_tp,) + g.shape), "tp").reshape(-1, dim)
    shard = jax.ops.segment_sum(g_all, jnp.where(owned, local, rows), num_segments=rows, mode="drop")
    emb = jnp.sum(swap(shard.reshape(n_dp, out_rows, -1), "dp"), axis=0) * scale
    return x_emb, y_norm, emb, w


def route(n_dp, n_tp, out_rows, ids):
    plane = lax.axis_index("tp")
    n = ids.shape[0]
    shard_rows = n_dp * out_rows
    local = ids - plane * shard_rows
    owned = (local >= 0) & (local < shard_rows)
    far = owned & (local >= FRONT)
    cold = ids >= HOT
    mine = cold & owned
    blk = (ids // out_rows) % n_dp
    marks = jnp.concatenate([(blk[:, None] == jnp.arange(n_dp)[None]) & mine[:, None], far[:, None]], axis=1)
    before = (jnp.arange(n)[:, None] > jnp.arange(n)[None]).astype(BF16)
    ranks = jnp.dot(before, marks.astype(BF16), preferred_element_type=F32)
    rank = jnp.sum(jnp.where(marks, ranks, 0.0)[:, :n_dp], axis=1).astype(I32)
    far_rank = ranks[:, n_dp].astype(I32)
    comb = jnp.where(far, FRONT + far_rank * 2 + (local & 1), jnp.where(owned, local, -1))
    hit = (jnp.arange(FAR)[:, None] == far_rank[None]) & far[None]
    pair = jnp.max(jnp.where(hit, (local >> 1)[None], 0), axis=1)
    count = jnp.sum(far.astype(I32)).reshape(1)
    cold_slot = slot_base(plane, blk) + hot_rows(plane) + rank
    per_plane = n_dp * HOT_ROWS
    in_plane = ids % per_plane
    hot_slot = slot_base(plane, in_plane // HOT_ROWS) + in_plane % HOT_ROWS
    hot = jnp.logical_not(cold) & (ids // per_plane == plane - HOT_PLANE)
    slot = jnp.where(mine, cold_slot, jnp.where(hot, hot_slot, -1))
    d, c = jnp.arange(n_dp)[:, None], jnp.arange(STRIDE)[None]
    size = hot_rows(plane) + cold_cap(plane, d)
    at = jnp.where(c < size, slot_base(plane, d) + c, -2).reshape(-1)
    row = jnp.max(jnp.where((at[:, None] == slot[None]) & mine[None], (ids % out_rows)[None], -1), axis=1)
    row = row.reshape(n_dp, 1, STRIDE)
    row = jnp.concatenate([row, row], axis=2)
    bin_no = jnp.arange(n_dp * n_tp)
    hits = ((ids // out_rows)[:, None] == bin_no[None]) & cold[:, None]
    flag = jnp.any(jnp.sum(hits.astype(I32), axis=0) > cold_cap(bin_no // n_dp, bin_no % n_dp))
    all_far = ((ids // shard_rows)[:, None] == jnp.arange(n_tp)[None]) & (ids % shard_rows >= FRONT)[:, None]
    flag = flag | jnp.any(jnp.sum(all_far.astype(I32), axis=0) > FAR)
    send = jnp.where(jnp.arange(8)[None, :, None] == 1, flag.astype(I32), row)
    return comb.reshape(n, 1), pair, count, slot.reshape(1, n), send


def solution(mesh):
    n_dp, n_tp = mesh.shape["dp"], mesh.shape["tp"]

    def local_step(tokens, emb_table, w_norm, dy_norm, dy_resid):
        out_rows = emb_table.shape[0] // n_dp
        ids = tokens[0]
        comb, pair, count, slot, send_idx = route(n_dp, n_tp, out_rows, ids)
        far = far_rows(emb_table, pair, count)
        *fast, idx = fused_step(n_dp, n_tp, out_rows, comb, far, emb_table, slot, send_idx, w_norm, dy_norm[0], dy_resid[0])
        fits = jnp.max(idx[:, 1, :]) == 0
        x_emb, y_norm, emb_grad, w_sum = lax.cond(
            fits,
            lambda: tuple(fast),
            lambda: dense_step(n_dp, n_tp, out_rows, ids, emb_table, w_norm, dy_norm[0], dy_resid[0]),
        )
        return x_emb[None], y_norm[None], emb_grad, w_sum[0]

    act_spec = P("dp", "tp", None)
    return jax.shard_map(local_step, mesh=mesh, in_specs=(P("dp", None), P("tp", None), P(None), act_spec, act_spec), out_specs=(act_spec, act_spec, P(("tp", "dp"), None), P(None)), check_vma=False)
```

time: 188 us -> 165 us (0.88)
  Pallas kernels: 162 us -> 135 us
  other arithmetic: 9.99 us -> 11.9 us
    pallas_call x2, Pallas kernels: 162 us -> 135 us  [the longest x1 130 us: fused_step(): pl.pallas_call(functools.partial(step_kernel, n_dp, n_tp), grid=(1,), out...]
    unnamed x13 -> x10, local copies, waits for them, and re-layouts: 10.7 us -> 11.1 us
where the time goes in v4:
time: 165 us; the launch traced here: 164 us
  Pallas kernels  135 us (82%)
  local copies, waits for them, and re-layouts  12.9 us (8%)
  other arithmetic  11.9 us (7%)
  between operations  2.74 us (2%)
    pallas_call x1, Pallas kernels, fused_step(): pl.pallas_call(functools.partial(step_kernel, n_dp, n_tp), grid=(1,), out...  130 us
    unnamed x10, local copies, waits for them, and re-layouts  11.1 us
    pallas_call x1, Pallas kernels, far_rows(): pl.pallas_call(far_kernel, out_shape=jax.ShapeDtypeStruct((2 * FAR, table...  5.05 us

profile of v4, /device:TPU:0, one launch (start us, length us, event | category | flops | bytes accessed | tf_op | source)
XLA Modules:
  0.0 163.8 jit_solution(602314306706397672)
XLA Ops:
  0.7 0.7 fusion.41
  1.4 0.7 fusion.20
  2.1 0.1 add_select_fusion
  2.2 0.1 select_n.342
  2.3 1.3 reshape.371.gain_ref
  3.6 0.7 and_select_fusion.2
  4.3 1.3 add_select_fusion.2
  5.6 0.3 convert_reduce_fusion
  6.0 0.6 compare_reduce_fusion.1
  6.6 0.1 convert_reduce_fusion.2
  6.7 0.6 compare_reduce_fusion
  8.7 0.2 copy.27
  8.9 0.1 compare_and_fusion
  9.1 0.2 copy.30
  9.3 0.5 fusion.9
  9.8 0.8 fusion.23.slot_ref
  10.7 0.6 copy-done.5
  11.3 1.1 select_reduce_fusion
  12.4 0.1 add_bitcast_fusion
  12.5 0.7 broadcast_select_fusion.send_ref
  13.2 0.2 copy.36
  13.4 1.0 convert_reduce_fusion.1
  14.5 0.4 select_reduce_fusion.1.blk_ref
  14.9 5.1 %far_rows.1.far_ref = bf16[640,2304]{1,0:T(8,128)(2,1)S(1)} custom-call(s32[320]{0:T(512)S(1)} %select_reduce_fusion.1.blk_ref, s32[1]{0:T(128)} %bitcast.14.count_ref, bf16[8192,2304]{1,0:T(8,128)(2,1)} %front_ref.1), custom_call_target="tpu_custom_call" | custom-call | tf_op jit(solution)/shard_map/far_rows/pallas_call | solution.py:61
  19.9 1.6 copy-done
  21.5 130.4 %fused_step.1 = (bf16[128,2304]{1,0:T(8,128)(2,1)}, bf16[128,2304]{1,0:T(8,128)(2,1)}, f32[512,2304]{1,0:T(8,128)}, f32[1,2304]{1,0:T(1,128)}, s32[16,8,128]{2,1,0:T(8,128)}) custom-call(s32[1024,1]{1,0:T(8,128)} %get-tuple-element.65.comb_ref, bf16[640,2304]{1,0:T(8,128)(2,1)} %copy-done, bf16[8192,2304]{1,0:T(8,128)(2,1)} %front_ref.1, ...), custom_call_target="tpu_custom_call" | custom-call | tf_op jit(solution)/shard_map/fused_step/pallas_call | solution.py:463
  152.0 1.5 slice_reduce_fusion
  154.1 1.0 conditional.1
  154.4 0.7 reduce.3
  155.1 1.9 %copy.49 = bf16[1,128,2304]{2,1,0:T(8,128)(2,1)} copy(bf16[1,128,2304]{2,1,0:T(8,128)(2,1)} %get-tuple-element.94) | data formatting | bytes 1179648
  157.0 1.9 %copy.50 = bf16[1,128,2304]{2,1,0:T(8,128)(2,1)} copy(bf16[1,128,2304]{2,1,0:T(8,128)(2,1)} %get-tuple-element.95) | data formatting | bytes 1179648
  158.9 4.8 %copy.51 = f32[512,2304]{1,0:T(8,128)} copy(f32[512,2304]{1,0:T(8,128)} %get-tuple-element.96) | data formatting | bytes 9437184
  (11 shorter events, 0.2 us)
Async XLA Ops:
  10.7 0.6 copy-start.5
  19.9 1.6 copy-start
  155.1 8.7 %copy-start.6 = (f32[2304]{0:T(1024)}, f32[2304]{0:T(1024)S(1)}, u32[]{:S(2)}) copy-start(f32[2304]{0:T(1024)S(1)} %get-tuple-element.97) | copy-start | bytes 27652

commit v5 on v4

--- a/solution.py
+++ b/solution.py
@@ -39,35 +39,147 @@
     return jnp.where(tp == 0, first, (16 + hot_rows(tp)) * blk)
 
 
-def far_kernel(blk_ref, count_ref, table_ref, out_ref, sem):
-    count = jnp.minimum(count_ref[0], FAR)
-    out_ref[...] = jnp.zeros(out_ref.shape, BF16)
-
-    def copy(i):
+def plan_kernel(n_dp, n_tp, ids_ref, table_ref, comb_ref, far_ref, slot_ref, send_ref,
+                before, hits, pairs, pairs_smem, sem, far_sem):
+    plane = lax.axis_index("tp")
+    n = ids_ref.shape[1]
+    shard_rows = table_ref.shape[0]
+    out_rows = shard_rows // n_dp
+    ids = ids_ref[...]
+    local = ids - plane * shard_rows
+    owned = jnp.logical_and(local >= 0, local < shard_rows)
+    far = jnp.logical_and(owned, local >= FRONT)
+    cold = ids >= HOT
+    mine = jnp.logical_and(cold, owned)
+    bins = lax.div(ids, out_rows)
+    blk = lax.rem(bins, n_dp)
+    far_ref[...] = jnp.zeros(far_ref.shape, BF16)
+
+    @pl.loop(0, n // 128)
+    def _(b):
+        base = pl.multiple_of(b * 128, 128)
+        row = lax.broadcasted_iota(I32, (128, n), 0) + base
+        before[pl.ds(base, 128), :] = (row < lax.broadcasted_iota(I32, (128, n), 1)).astype(BF16)
+
+    kind = lax.broadcasted_iota(I32, (2 * n_dp, n), 0)
+    mark = jnp.logical_or(jnp.logical_and(kind == blk, mine), jnp.logical_and(kind == n_dp, far))
+    ranks = jnp.dot(mark.astype(BF16), before[...], preferred_element_type=F32)
+    rank = jnp.sum(jnp.where(jnp.logical_and(mark, kind < n_dp), ranks, 0.0), axis=0, keepdims=True).astype(I32)
+    far_rank = jnp.sum(jnp.where(jnp.logical_and(mark, kind == n_dp), ranks, 0.0), axis=0, keepdims=True).astype(I32)
+    count = jnp.sum(far.astype(F32))
+
+    comb = jnp.where(far, FRONT + far_rank * 2 + lax.rem(local, 2), jnp.where(owned, local, -1))
+    place = hot_rows(plane) + rank
+    per_plane = n_dp * HOT_ROWS
+    in_plane = lax.rem(ids, per_plane)
+    hot_slot = slot_base(plane, lax.div(in_plane, HOT_ROWS)) + lax.rem(in_plane, HOT_ROWS)
+    hot = jnp.logical_and(jnp.logical_not(cold), lax.div(ids, per_plane) == plane - HOT_PLANE)
+    slot_ref[...] = jnp.where(mine, slot_base(plane, blk) + place, jnp.where(hot, hot_slot, -1))
+
+    wide_slot = jnp.where(jnp.logical_and(mine, place < STRIDE), blk * STRIDE + place, -1)
+    far_slot = jnp.where(far, far_rank, -1)
+    sub = lax.broadcasted_iota(I32, (8, n), 0)
+    stack = jnp.where(sub == 0, comb, jnp.where(sub == 1, wide_slot, jnp.where(sub == 2, far_slot, bins)))
+    stack = jnp.where(jnp.logical_and(sub == 4, jnp.logical_not(cold)), -1, stack)
+    in_front = lax.rem(ids, shard_rows) < FRONT
+    stack = jnp.where(sub == 5, jnp.where(in_front, -1, lax.div(ids, shard_rows)), stack)
+    cols = jnp.transpose(stack.astype(F32)).astype(I32)
+    comb_ref[...] = cols
+
+    half = lax.div(local, 2)
+    row = lax.rem(ids, out_rows)
+    vals = jnp.where(sub == 0, lax.rem(half, 64), jnp.where(sub == 1, lax.div(half, 64), jnp.where(
+        sub == 2, lax.rem(row, 16), jnp.where(sub == 3, lax.div(row, 16), 1))))
+    vals = vals.astype(F32).astype(BF16)
+
+    def pull(at, width):
+        @pl.loop(0, n // 128)
+        def _(b):
+            rows = pl.ds(pl.multiple_of(b * 128, 128), 128)
+            lane = lax.broadcasted_iota(I32, (128, width), 1)
+            hits[rows, :width] = (lane == comb_ref[rows, at:at + 1]).astype(BF16)
+        return jnp.dot(vals, hits[:, :width], preferred_element_type=F32)
+
+    found = pull(2, pairs.shape[1])
+    pick = found[1:2, :] * 64.0 + found[0:1, :]
+    which = lax.broadcasted_iota(I32, pairs.shape, 0)
+    pairs[...] = jnp.where(which == 0, pick, jnp.minimum(count, 1.0 * FAR)).astype(I32)
+    move = pltpu.make_async_copy(pairs, pairs_smem, sem)
+    move.start()
+    move.wait()
+    n_far = pairs_smem[1, 0]
+
+    def far_copy(src, i):
         return pltpu.make_async_copy(
-            table_ref.at[pl.ds(pl.multiple_of(blk_ref[i] * 2, 2), 2), :],
-            out_ref.at[pl.ds(pl.multiple_of(i * 2, 2), 2), :], sem)
-
-    @pl.loop(0, count)
+            table_ref.at[pl.ds(pl.multiple_of(src * 2, 2), 2), :],
+            far_ref.at[pl.ds(pl.multiple_of(i * 2, 2), 2), :], far_sem)
+
+    @pl.loop(0, n_far)
     def _(i):
-        copy(i).start()
-
-    @pl.loop(0, count)
+        far_copy(pairs_smem[0, i], i).start()
+
+    found = pull(1, n_dp * STRIDE)
+    taken = found[4:5, :] > 0.5
+    idx = jnp.where(taken, (found[3:4, :] * 16.0 + found[2:3, :]).astype(I32), -1)
+
+    lane = lax.broadcasted_iota(I32, (n, 128), 1)
+    in_bin = jnp.sum(jnp.where(lane == cols[:, 4:5], 1.0, 0.0), axis=0, keepdims=True)
+    in_far = jnp.sum(jnp.where(lane == cols[:, 5:6], 1.0, 0.0), axis=0, keepdims=True)
+    bin_no = lax.broadcasted_iota(I32, (1, 128), 1)
+    cap = cold_cap(lax.div(bin_no, n_dp), lax.rem(bin_no, n_dp)).astype(F32)
+    over = jnp.logical_or(in_bin > cap, in_far > 1.0 * FAR)
+    flag = jnp.broadcast_to(jnp.max(jnp.where(over, 1.0, 0.0), axis=1, keepdims=True), (1, 128)).astype(I32)
+    which = lax.broadcasted_iota(I32, (8, 128), 0)
+    for p in range(n_dp // 2):
+        send_ref[p] = jnp.where(which == 1, flag, idx[:, p * 128:(p + 1) * 128])
+
+    @pl.loop(0, n_far)
     def _(i):
-        copy(0).wait()
-
-
-def far_rows(table, blk, count):
+        far_copy(0, i).wait()
+
+
+def make_plan(n_dp, n_tp, ids, table):
+    n = ids.shape[1]
+    vmem = pl.BlockSpec(memory_space=VMEM)
+    shape = jax.ShapeDtypeStruct
+    dma = pltpu.SemaphoreType.DMA
+    n_pairs = FAR + -FAR % 128
     return pl.pallas_call(
-        far_kernel,
-        out_shape=jax.ShapeDtypeStruct((2 * FAR, table.shape[1]), BF16),
-        in_specs=[pl.BlockSpec(memory_space=pltpu.SMEM), pl.BlockSpec(memory_space=pltpu.SMEM),
-                  pl.BlockSpec(memory_space=ANY)],
-        out_specs=pl.BlockSpec(memory_space=VMEM),
-        scratch_shapes=[pltpu.SemaphoreType.DMA],
-        compiler_params=pltpu.CompilerParams(vmem_limit_bytes=16 * 2**20),
-        name="far_rows",
-    )(blk, count, table)
+        functools.partial(plan_kernel, n_dp, n_tp),
+        out_shape=(shape((n, 8), I32), shape((2 * FAR, table.shape[1]), BF16),
+                   shape((1, n), I32), shape((n_dp // 2, 8, 128), I32)),
+        in_specs=[vmem, pl.BlockSpec(memory_space=ANY)],
+        out_specs=(vmem,) * 4,
+        scratch_shapes=[
+            VMEM((n, n), BF16),
+            VMEM((n, n_dp * STRIDE), BF16),
+            VMEM((8, n_pairs), I32),
+            pltpu.SMEM((8, n_pairs), I32),
+            dma, dma,
+        ],
+        compiler_params=pltpu.CompilerParams(vmem_limit_bytes=24 * 2**20),
+        name="make_plan",
+    )(ids, table)
+
+
+def copy_kernel(x_ref, y_ref, e_ref, xo_ref, yo_ref, eo_ref):
+    xo_ref[...] = x_ref[...]
+    yo_ref[...] = y_ref[...]
+    eo_ref[...] = e_ref[...]
+
+
+def hand_on(x, y, e):
+    steps = 8
+    specs = [pl.BlockSpec((a.shape[0] // steps, a.shape[1]), lambda i: (i, 0)) for a in (x, y, e)]
+    return pl.pallas_call(
+        copy_kernel,
+        grid=(steps,),
+        out_shape=tuple(jax.ShapeDtypeStruct(a.shape, a.dtype) for a in (x, y, e)),
+        in_specs=specs,
+        out_specs=tuple(specs),
+        compiler_params=pltpu.CompilerParams(vmem_limit_bytes=8 * 2**20),
+        name="hand_on",
+    )(x, y, e)
 
 
 class Line:
@@ -112,8 +224,8 @@
 
 
 def step_kernel(n_dp, n_tp, comb_ref, far_ref, front_ref, slot_ref, send_ref, gain_ref, dyn_ref, dyr_ref,
-                x_ref, y_ref, out_ref, wout_ref, idx_ref,
-                sel, mine, chip_sum, half_in, full_in, g_ref, g_all, pick, place, send, recv, hot_send, hot_recv,
+                x_ref, y_ref, out_ref, wout_ref, flag_ref,
+                idx_ref, sel, mine, chip_sum, half_in, full_in, g_ref, g_all, pick, place, send, recv, hot_send, hot_recv,
                 w_acc, w_part, w_dp, w_sum, w_tp,
                 d_send, d_recv, h_send, h_recv, f_send, f_recv, i_send, i_recv,
                 ag_send, ag_recv, a_send, a_recv, hot_out, hot_in, wd_send, wd_recv, wt_send, wt_recv):
@@ -161,7 +273,7 @@
 
     def idx_copy(i, to, slot):
         return pltpu.make_async_remote_copy(
-            src_ref=send_ref.at[to], dst_ref=idx_ref.at[slot], send_sem=i_send.at[i], recv_sem=i_recv.at[i],
+            src_ref=send_ref.at[lax.div(to, 2)], dst_ref=idx_ref.at[slot], send_sem=i_send.at[i], recv_sem=i_recv.at[i],
             device_id={"dp": to}, device_id_type=MESH)
 
     for i in range(1, n_dp):
@@ -175,7 +287,7 @@
         mine_tp = line.chips[order[k]]
         for part, tp in enumerate((line.other(mine_tp), mine_tp)):
             lanes = lax.broadcasted_iota(I32, (n_pos, sel.shape[1]), 1)
-            sel[pl.ds(part * n_pos, n_pos), :] = (lanes == comb_ref[block(tp), :]).astype(BF16)
+            sel[pl.ds(part * n_pos, n_pos), :] = (lanes == comb_ref[block(tp), :1]).astype(BF16)
 
         @pl.loop(0, NCHUNK)
         def _(c):
@@ -241,16 +353,24 @@
         def _(r):
             recv[s, pl.ds(pl.multiple_of(r * 8, 8), 8), :] = jnp.zeros((8, dim), F32)
 
-    idx_ref[pl.ds(me, 1)] = send_ref[pl.ds(me, 1)]
+    idx_ref[pl.ds(me, 1)] = send_ref[pl.ds(lax.div(me, 2), 1)]
     for i in range(1, n_dp):
         to, frm = peer(i)
         idx_copy(i, to, me).wait_send()
         idx_copy(i, frm, frm).wait_recv()
 
+    flag_ref[...] = jnp.max(idx_ref[...], axis=0)
+
     @pl.loop(0, n_dp // 2)
     def _(p):
-        lane = lax.broadcasted_iota(I32, (1, 128), 1)
-        idx = jnp.where(lane < STRIDE, idx_ref[2 * p, 0:1, :], idx_ref[2 * p + 1, 0:1, :])
+        upper = lax.broadcasted_iota(I32, (1, 128), 1) >= STRIDE
+        here = (lax.rem(me, 2) == 1)
+
+        def for_me(s):
+            v = idx_ref[s, 0:1, :]
+            return jnp.where(jnp.logical_xor(upper, here), pltpu.roll(v, STRIDE, 1), v)
+
+        idx = jnp.where(upper, for_me(2 * p + 1), for_me(2 * p))
         rows = lax.broadcasted_iota(I32, (place.shape[0], 128), 0)
         place[:, pl.ds(pl.multiple_of(p * 128, 128), 128)] = (rows == idx).astype(BF16)
 
@@ -464,10 +584,11 @@
         functools.partial(step_kernel, n_dp, n_tp),
         grid=(1,),
         out_shape=(shape((n_pos, dim), BF16), shape((n_pos, dim), BF16),
-                   shape((out_rows, dim), F32), shape((1, dim), F32), shape(send_idx.shape, I32)),
+                   shape((out_rows, dim), F32), shape((1, dim), F32), shape((8, 128), I32)),
         in_specs=[vmem, vmem, pl.BlockSpec((FRONT, dim), lambda i: (0, 0), pipeline_mode=pl.Buffered(1))] + [vmem] * 5,
         out_specs=(vmem,) * 5,
         scratch_shapes=[
+            VMEM((n_dp, 8, 128), I32),
             VMEM((2 * n_pos, FRONT + 2 * FAR), BF16),
             VMEM((4, n_pos, dim), F32),
             VMEM((4, n_pos, dim), F32),
@@ -527,59 +648,18 @@
     return x_emb, y_norm, emb, w
 
 
-def route(n_dp, n_tp, out_rows, ids):
-    plane = lax.axis_index("tp")
-    n = ids.shape[0]
-    shard_rows = n_dp * out_rows
-    local = ids - plane * shard_rows
-    owned = (local >= 0) & (local < shard_rows)
-    far = owned & (local >= FRONT)
-    cold = ids >= HOT
-    mine = cold & owned
-    blk = (ids // out_rows) % n_dp
-    marks = jnp.concatenate([(blk[:, None] == jnp.arange(n_dp)[None]) & mine[:, None], far[:, None]], axis=1)
-    before = (jnp.arange(n)[:, None] > jnp.arange(n)[None]).astype(BF16)
-    ranks = jnp.dot(before, marks.astype(BF16), preferred_element_type=F32)
-    rank = jnp.sum(jnp.where(marks, ranks, 0.0)[:, :n_dp], axis=1).astype(I32)
-    far_rank = ranks[:, n_dp].astype(I32)
-    comb = jnp.where(far, FRONT + far_rank * 2 + (local & 1), jnp.where(owned, local, -1))
-    hit = (jnp.arange(FAR)[:, None] == far_rank[None]) & far[None]
-    pair = jnp.max(jnp.where(hit, (local >> 1)[None], 0), axis=1)
-    count = jnp.sum(far.astype(I32)).reshape(1)
-    cold_slot = slot_base(plane, blk) + hot_rows(plane) + rank
-    per_plane = n_dp * HOT_ROWS
-    in_plane = ids % per_plane
-    hot_slot = slot_base(plane, in_plane // HOT_ROWS) + in_plane % HOT_ROWS
-    hot = jnp.logical_not(cold) & (ids // per_plane == plane - HOT_PLANE)
-    slot = jnp.where(mine, cold_slot, jnp.where(hot, hot_slot, -1))
-    d, c = jnp.arange(n_dp)[:, None], jnp.arange(STRIDE)[None]
-    size = hot_rows(plane) + cold_cap(plane, d)
-    at = jnp.where(c < size, slot_base(plane, d) + c, -2).reshape(-1)
-    row = jnp.max(jnp.where((at[:, None] == slot[None]) & mine[None], (ids % out_rows)[None], -1), axis=1)
-    row = row.reshape(n_dp, 1, STRIDE)
-    row = jnp.concatenate([row, row], axis=2)
-    bin_no = jnp.arange(n_dp * n_tp)
-    hits = ((ids // out_rows)[:, None] == bin_no[None]) & cold[:, None]
-    flag = jnp.any(jnp.sum(hits.astype(I32), axis=0) > cold_cap(bin_no // n_dp, bin_no % n_dp))
-    all_far = ((ids // shard_rows)[:, None] == jnp.arange(n_tp)[None]) & (ids % shard_rows >= FRONT)[:, None]
-    flag = flag | jnp.any(jnp.sum(all_far.astype(I32), axis=0) > FAR)
-    send = jnp.where(jnp.arange(8)[None, :, None] == 1, flag.astype(I32), row)
-    return comb.reshape(n, 1), pair, count, slot.reshape(1, n), send
-
-
 def solution(mesh):
     n_dp, n_tp = mesh.shape["dp"], mesh.shape["tp"]
 
     def local_step(tokens, emb_table, w_norm, dy_norm, dy_resid):
         out_rows = emb_table.shape[0] // n_dp
         ids = tokens[0]
-        comb, pair, count, slot, send_idx = route(n_dp, n_tp, out_rows, ids)
-        far = far_rows(emb_table, pair, count)
-        *fast, idx = fused_step(n_dp, n_tp, out_rows, comb, far, emb_table, slot, send_idx, w_norm, dy_norm[0], dy_resid[0])
-        fits = jnp.max(idx[:, 1, :]) == 0
+        comb, far, slot, send_idx = make_plan(n_dp, n_tp, tokens, emb_table)
+        *fast, w_fast, flag = fused_step(n_dp, n_tp, out_rows, comb, far, emb_table, slot, send_idx, w_norm, dy_norm[0], dy_resid[0])
+        fits = flag[1, 0] == 0
         x_emb, y_norm, emb_grad, w_sum = lax.cond(
             fits,
-            lambda: tuple(fast),
+            lambda: (*hand_on(*fast), w_fast),
             lambda: dense_step(n_dp, n_tp, out_rows, ids, emb_table, w_norm, dy_norm[0], dy_resid[0]),
         )
         return x_emb[None], y_norm[None], emb_grad, w_sum[0]

time: 165 us -> 155 us (0.939)
  other arithmetic: 11.9 us -> 0.03 us
  Pallas kernels: 135 us -> 146 us
  local copies, waits for them, and re-layouts: 12.9 us -> 5.99 us
    pallas_call x1 -> x2, Pallas kernels: 5.05 us -> 16.5 us  [the longest x1 8.85 us: make_plan(): pl.pallas_call(functools.partial(plan_kernel, n_dp, n_tp), out_shape=(sha...]
    unnamed x10 -> x12, local copies, waits for them, and re-layouts: 11.1 us -> 4.19 us
    select_n x6 -> x0, other arithmetic: 3.67 us -> none  [the longest x1 1.33 us: route(): ids // shard_rows]
    reduce_max x3 -> x0, other arithmetic: 2.98 us -> none  [the longest x1 1.49 us: local_step(): fits = jnp.max(idx[:, 1, :]) == 0]
where the time goes in v5:
time: 155 us; the launch traced here: 154 us
  Pallas kernels  146 us (94%)
  local copies, waits for them, and re-layouts  5.99 us (4%)
    pallas_call x1, Pallas kernels, fused_step(): pl.pallas_call(functools.partial(step_kernel, n_dp, n_tp), grid=(1,), out...  130 us
    pallas_call x1, Pallas kernels, make_plan(): pl.pallas_call(functools.partial(plan_kernel, n_dp, n_tp), out_shape=(sha...  8.85 us
    pallas_call x1, Pallas kernels, hand_on(): pl.pallas_call(copy_kernel, grid=(steps,), out_shape=tuple((jax.ShapeDtyp...  7.66 us
    unnamed x12, local copies, waits for them, and re-layouts  4.19 us

profile of v5, /device:TPU:0, one launch (start us, length us, event | category | flops | bytes accessed | tf_op | source)
XLA Modules:
  0.0 154.1 jit_solution(15580474378151379013)
XLA Ops:
  0.6 0.0 copy-start.7
  0.6 8.9 %make_plan.1 = (s32[1024,8]{1,0:T(8,128)S(1)}, bf16[640,2304]{1,0:T(8,128)(2,1)S(1)}, s32[1,1024]{1,0:T(1,128)S(1)}, s32[8,8,128]{2,1,0:T(8,128)S(1)}) custom-call(s32[1,1024]{1,0:T(1,128)} %ids_ref.1, bf16[8192,2304]{1,0:T(8,128)(2,1)} %front_ref.1), custom_call_target="tpu_custom_call" | custom-call | tf_op jit(solution)/shard_map/make_plan/pallas_call | solution.py:147
  9.5 0.0 copy-start
  9.5 1.6 %copy-done = bf16[640,2304]{1,0:T(8,128)(2,1)} copy-done((bf16[640,2304]{1,0:T(8,128)(2,1)}, bf16[640,2304]{1,0:T(8,128)(2,1)S(1)}, u32[]{:S(2)}) %copy-start) | copy-done | bytes 2949144
  11.1 0.0 copy-start.1
  11.1 0.8 copy-done.1
  11.9 0.0 copy-start.2
  11.9 0.6 copy-done.2
  12.5 0.0 copy-start.3
  12.5 0.6 copy-done.3
  13.1 0.0 copy-done.7
  13.1 0.6 reshape.105.gain_ref
  13.7 130.0 %fused_step.1 = (bf16[128,2304]{1,0:T(8,128)(2,1)}, bf16[128,2304]{1,0:T(8,128)(2,1)}, f32[512,2304]{1,0:T(8,128)}, f32[1,2304]{1,0:T(1,128)}, s32[8,128]{1,0:T(8,128)}) custom-call(s32[1024,8]{1,0:T(8,128)} %copy-done.1, bf16[640,2304]{1,0:T(8,128)(2,1)} %copy-done, bf16[8192,2304]{1,0:T(8,128)(2,1)} %front_ref.1, s32[1,1024]{1,0:T(1,128)} %copy-done.3, ...), custom_call_target="tpu_custom_call" | custom-call | tf_op jit(solution)/shard_map/fused_step/pallas_call | solution.py:583
  143.7 1.2 slice.3
  145.5 7.9 %conditional.1 = (f32[512,2304]{1,0:T(8,128)}, bf16[1,128,2304]{2,1,0:T(8,128)(2,1)}, bf16[1,128,2304]{2,1,0:T(8,128)(2,1)}, f32[2304]{0:T(1024)S(1)}) conditional(s32[]{:T(128)} %bitcast.15, (s32[1,1024]{1,0:T(1,128)}, bf16[1,128,2304]{2,1,0:T(8,128)(2,1)}, bf16[8192,2304]{1,0:T(8,128)(2,1)}, bf16[1,128,2304]{2,1,0:T(8,128)(2,1)}, ...), branch_computations={%region_0.9_spmd, %region_9.10_spmd} | conditional | flops 39884420 | bytes 535068000 | solution.py:660
  145.8 0.0 copy-start.10
  145.8 7.7 %hand_on.1 = (bf16[128,2304]{1,0:T(8,128)(2,1)}, bf16[128,2304]{1,0:T(8,128)(2,1)}, f32[512,2304]{1,0:T(8,128)}) custom-call(bf16[128,2304]{1,0:T(8,128)(2,1)} %get-tuple-element.26.x_ref, bf16[128,2304]{1,0:T(8,128)(2,1)} %get-tuple-element.27.y_ref, f32[512,2304]{1,0:T(8,128)} %get-tuple-element.28.e_ref), custom_call_target="tpu_custom_call" | custom-call | tf_op jit(solution)/shard_map/cond/branch_1_fun/hand_on/pallas_call | solution.py:174
  153.4 0.0 copy-done.10
  153.5 0.0 copy-start.9
  153.5 0.6 copy-done.9
  (1 shorter events, 0.0 us)
Async XLA Ops:
  0.6 12.5 %copy-start.7 = (f32[2304]{0:T(1024)S(1)}, f32[2304]{0:T(1024)}, u32[]{:S(2)}) copy-start(f32[2304]{0:T(1024)} %param.9) | copy-start | bytes 27652
  9.5 1.6 %copy-start = (bf16[640,2304]{1,0:T(8,128)(2,1)}, bf16[640,2304]{1,0:T(8,128)(2,1)S(1)}, u32[]{:S(2)}) copy-start(bf16[640,2304]{1,0:T(8,128)(2,1)S(1)} %get-tuple-element.51.far_ref) | copy-start | bytes 8847364
  11.1 0.8 copy-start.1
  11.9 0.6 copy-start.2
  12.5 0.6 copy-start.3
  145.8 7.7 %copy-start.10 = (f32[1,2304]{1,0:T(1,128)S(1)}, f32[1,2304]{1,0:T(1,128)}, u32[]{:S(2)}) copy-start(f32[1,2304]{1,0:T(1,128)} %get-tuple-element.32) | copy-start | bytes 27652 | tf_op jit(solution)/shard_map/cond
  153.5 0.6 copy-start.9
